TPU v7x, 128 devices: a whole 4x4x4 slice. The times are simulated.
128 devices in a mesh: ha: 4 (over z_lo, core), wa: 4 (over y), hd: 8 (over z_hi, x).
Axes of the slice: x: 4, y: 4, z: 4 (z_hi: 2, z_lo: 2; z = z_hi * 2 + z_lo), core: 2. Of those that a mesh axis runs over, the one named last changes fastest.
Arguments:
- queries: bfloat16 [12, 32, 64, 3072], P(None, 'ha', 'wa', 'hd'), may hold values from -10 to 10
- video_keys: bfloat16 [12, 32, 64, 3072], P(None, 'ha', 'wa', 'hd'), may hold values from -5 to 5
- video_values: bfloat16 [12, 32, 64, 3072], P(None, 'ha', 'wa', 'hd'), may hold values from -6 to 6
- text_keys: bfloat16 [256, 3072], P(None, 'hd'), may hold values from -5 to 5
- text_values: bfloat16 [256, 3072], P(None, 'hd'), may hold values from -6 to 6
- tile_radius: int32 [3, 2, 4, 8], P(None, None, 'ha', 'wa'), may hold values from 0 to 1, as said below
- out_weight: bfloat16 [3072, 3072], P('hd'), may hold values from -0.875 to 0.875
Outputs:
- projected: bfloat16 [12, 32, 64, 3072], P(None, 'ha', 'wa', 'hd')
Inputs may be any that keep to these rules, and one draw needn't show every extreme that they name: `tile_radius`: every video query has a window of at most one tile in each direction; some tile has radius 1 in all three.
All inputs are finite; a program needn't handle non-finite values.
Results may differ from a plain program's by a relative error of at most 0.012.
Values may be sent and summed in bfloat16 or wider, within the bound.
A program may use at most 192 MiB of HBM per device.

v0:
```python
import jax
import jax.numpy as jnp
from jax import lax
from jax.sharding import PartitionSpec as P

HEAD = 128
TILE_T = 6
TILE_H = 8
TILE_W = 8


def extended(block, sides, width):
    for axis, dim in sides:
        count = lax.axis_size(axis)
        forward = [(i, i + 1) for i in range(count - 1)]
        backward = [(target, source) for source, target in forward]
        low = lax.ppermute(
            lax.slice_in_dim(block, block.shape[dim] - width, None, axis=dim), axis, forward
        )
        high = lax.ppermute(lax.slice_in_dim(block, 0, width, axis=dim), axis, backward)
        block = jnp.concatenate([low, block, high], axis=dim)
    return block


def cut_along(value, dim, size):
    shape = value.shape
    blocks = value.reshape(*shape[:dim], size, shape[dim] // size, *shape[dim + 1 :])
    return jnp.moveaxis(blocks, dim, 0)


def summed_on_arrival(value, axis, dim):
    blocks = cut_along(value, dim, lax.axis_size(axis))
    arrived = lax.all_to_all(blocks, axis, split_axis=0, concat_axis=0, tiled=True)
    return arrived.astype(jnp.float32).sum(axis=0)


def attend(q_block, k_block, v_block, text_keys, text_values, allowed):
    head_count = q_block.shape[1] // HEAD
    factor = HEAD ** (-0.5)

    def one_head(head, result):
        offset = head * HEAD
        q_head = lax.dynamic_slice_in_dim(q_block, offset, HEAD, 1)
        k_head = lax.dynamic_slice_in_dim(k_block, offset, HEAD, 1)
        v_head = lax.dynamic_slice_in_dim(v_block, offset, HEAD, 1)
        tk_head = lax.dynamic_slice_in_dim(text_keys, offset, HEAD, 1)
        tv_head = lax.dynamic_slice_in_dim(text_values, offset, HEAD, 1)
        scores = (
            jnp.einsum("qd,kd->qk", q_head, k_head, preferred_element_type=jnp.float32) * factor
        )
        text_scores = (
            jnp.einsum("qd,kd->qk", q_head, tk_head, preferred_element_type=jnp.float32) * factor
        )
        row_peak = jnp.maximum(
            jnp.max(jnp.where(allowed, scores, -jnp.inf), axis=1), jnp.max(text_scores, axis=1)
        )[:, None]
        weights = jnp.where(allowed, jnp.exp(scores - row_peak), 0.0)
        text_weights = jnp.exp(text_scores - row_peak)
        row_total = jnp.sum(weights, axis=1) + jnp.sum(text_weights, axis=1)
        numerator = jnp.dot(
            weights.astype(jnp.bfloat16), v_head, preferred_element_type=jnp.float32
        )
        numerator = numerator + jnp.dot(
            text_weights.astype(jnp.bfloat16), tv_head, preferred_element_type=jnp.float32
        )
        head_out = (numerator / row_total[:, None]).astype(jnp.bfloat16)
        return lax.dynamic_update_slice_in_dim(result, head_out, offset, 1)

    return lax.fori_loop(0, head_count, one_head, jnp.zeros(q_block.shape, jnp.bfloat16))


def shards(queries, video_keys, video_values, text_keys, text_values, tile_radius, out_weight):
    n_frames, height, across, channels = queries.shape
    stacked = jnp.stack([video_keys, video_values])
    taller = extended(stacked, (("ha", 2),), TILE_H)
    padded = extended(taller, (("wa", 3),), TILE_W)
    row_tiles = height // TILE_H
    col_tiles = across // TILE_W
    all_rows = row_tiles * lax.axis_size("ha")
    all_cols = col_tiles * lax.axis_size("wa")
    row_base = lax.axis_index("ha") * row_tiles
    col_base = lax.axis_index("wa") * col_tiles
    padded_across = across + 2 * TILE_W
    key_frame = (jnp.arange(n_frames, dtype=jnp.int32) // TILE_T)[:, None, None]
    key_col = (col_base - 1 + jnp.arange(padded_across, dtype=jnp.int32) // TILE_W)[None, None, :]
    query_col = col_base + jnp.arange(across, dtype=jnp.int32) // TILE_W
    query_col = jnp.broadcast_to(query_col[None, None, :], (TILE_T, TILE_H, across)).reshape(-1)
    key_shape = (n_frames, 3 * TILE_H, padded_across)
    slabs = []
    for time_tile in range(n_frames // TILE_T):
        q_block = queries[time_tile * TILE_T : (time_tile + 1) * TILE_T, 0:TILE_H].reshape(
            -1, channels
        )
        window = padded.reshape(2, -1, channels)
        radii_row = jnp.repeat(tile_radius[:, time_tile, 0, :], TILE_W, axis=1)
        radii_query = jnp.broadcast_to(
            radii_row[:, None, None, :], (3, TILE_T, TILE_H, across)
        ).reshape(3, -1)
        here_row = row_base + 0
        key_row = (here_row - 1 + jnp.arange(3 * TILE_H, dtype=jnp.int32) // TILE_H)[None, :, None]
        key_valid = (key_row >= 0) & (key_row < all_rows) & (key_col >= 0) & (key_col < all_cols)
        key_valid = jnp.broadcast_to(key_valid, key_shape).reshape(-1)
        time_gap = jnp.broadcast_to(jnp.abs(key_frame - time_tile), key_shape).reshape(-1)
        row_gap = jnp.broadcast_to(jnp.abs(key_row - here_row), key_shape).reshape(-1)
        col_coord = jnp.broadcast_to(key_col, key_shape).reshape(-1)
        allowed = key_valid[None, :] & (time_gap[None, :] <= radii_query[0][:, None])
        allowed = allowed & (row_gap[None, :] <= radii_query[1][:, None])
        allowed = allowed & (
            jnp.abs(col_coord[None, :] - query_col[:, None]) <= radii_query[2][:, None]
        )
        attended = attend(q_block, window[0], window[1], text_keys, text_values, allowed)
        band_tiles = attended.reshape(TILE_T, TILE_H, across, channels)
        slabs.append(band_tiles)
    mixture = jnp.concatenate(slabs, axis=0)
    portion = jnp.dot(mixture.reshape(-1, channels), out_weight, preferred_element_type=jnp.float32)
    portion = portion.astype(jnp.bfloat16).reshape(n_frames, height, across, -1)
    return summed_on_arrival(portion, "hd", 3).astype(jnp.bfloat16)


def solution(mesh):
    placed = (
        P(None, "ha", "wa", "hd"),
        P(None, "ha", "wa", "hd"),
        P(None, "ha", "wa", "hd"),
        P(None, "hd"),
        P(None, "hd"),
        P(None, None, "ha", "wa"),
        P("hd", None),
    )
    return jax.shard_map(
        shards, mesh=mesh, in_specs=placed, out_specs=P(None, "ha", "wa", "hd"), check_vma=False
    )
```

profile of v0, /device:TPU:17, one launch (start us, length us, event | category | flops | bytes accessed | tf_op | source)
XLA Modules:
  0.0 682.4 jit_solution(13372110112280510802)
XLA Ops:
  8.2 23.8 %collective-permute-done = bf16[2,12,8,16,384]{4,3,2,1,0:T(8,128)(2,1)S(1)} collective-permute-done((bf16[2,12,8,16,384]{4,3,2,1,0:T(8,128)(2,1)S(1)}, bf16[2,12,8,16,384]{4,3,2,1,0:T(8,128)(2,1)S(1)}, u32[]{:S(2)}, u32[]{:S(2)}) %collective-permute-start) | collective-permute-done | bytes 2359328 | tf_op jit(solution)/shard_map/ppermute | solution.py:17
  86.2 15.5 %collective-permute-done.2 = bf16[2,12,24,8,384]{4,3,2,1,0:T(8,128)(2,1)} collective-permute-done((bf16[2,12,24,8,384]{4,3,2,1,0:T(8,128)(2,1)}, bf16[2,12,24,8,384]{4,3,2,1,0:T(8,128)(2,1)}, u32[]{:S(2)}, u32[]{:S(2)}) %collective-permute-start.2) | collective-permute-done | bytes 3538976 | tf_op jit(solution)/shard_map/ppermute | solution.py:17
  118.0 228.5 %while.28 = (s32[]{:T(128)}, bf16[768,384]{1,0:T(8,128)(2,1)}, bf16[768,384]{1,0:T(8,128)(2,1)}, bf16[9216,384]{1,0:T(8,128)(2,1)}, bf16[256,384]{1,0:T(8,128)(2...) while((s32[]{:T(128)}, bf16[768,384]{1,0:T(8,128)(2,1)}, ...), condition=%wide.region_5.6_spmd.clone, body=%wide.region_0.5_spmd.clone.sunk | while | flops 3973741056 | bytes 207235376 | solution.py:69
  118.2 23.0 %select_reduce_fusion.4 = (f32[768]{0:T(1024)S(1)}, f32[768,9216]{1,0:T(8,128)}) fusion(s32[768]{0:T(1024)} %get-tuple-element.754, s32[768]{0:T(1024)} %get-tuple-element.752, s32[9216]{0:T(1024)S(1)} %get-tuple-element.753, s32[768]{0:T(1024)} %get-tuple-element.750, s32[9216]{0:T(1024)S(1)} %get-tuple-element.751, s32[768]{0:T(1024)} %get-tuple-element.747, ...), kind=kOutput, calls=%fused_computation.4.clone.1 | convolution fusion | flops 1889795328 | bytes 31007744 | tf_op jit(solution)/shard_map/while/body/eval_jaxpr/qd,kd->qk/dot_general | solution.py:49
  142.6 24.7 %fusion.127 = f32[768]{0:T(1024)S(1)} fusion(f32[768,9216]{1,0:T(8,128)} %get-tuple-element.625, f32[768]{0:T(1024)S(1)} %max.26, s32[768]{0:T(1024)} %get-tuple-element.754, s32[768]{0:T(1024)} %get-tuple-element.752, s32[9216]{0:T(1024)S(1)} %get-tuple-element.753, s32[768]{0:T(1024)} %get-tuple-element.750, s32[9216]{0:T(1024)S(1)} %get-tuple-element.751, ...), kind=kLoop, calls=%fused_computation.6.clone.1 | loop fusion | flops 84933888 | bytes 28449792 | tf_op jit(solution)/shard_map/while/body/eval_jaxpr/reduce_sum | solution.py:59
  168.2 20.4 %fusion.129 = bf16[768,384]{1,0:T(8,128)(2,1)} fusion(bf16[768,384]{1,0:T(8,128)(2,1)} %get-tuple-element.722, s32[]{:T(128)S(6)} %select_n.177, f32[768,128]{1,0:T(8,128)S(1)} %fusion.126, bf16[9216,384]{1,0:T(8,128)(2,1)} %get-tuple-element.745, f32[768,9216]{1,0:T(8,128)S(1)} %copy-done.1, f32[768]{0:T(1024)} %copy-done.11, f32[768]{0:T(1024)} %add.240, ...), kind=kOutput, calls=%fused_computation.16.clone.1 | convolution fusion | flops 1897168896 | bytes 31406080 | tf_op jit(solution)/shard_map/while/body/eval_jaxpr/dot_general | solution.py:60
  188.6 22.9 %select_reduce_fusion.4 = (f32[768]{0:T(1024)S(1)}, f32[768,9216]{1,0:T(8,128)}) fusion(s32[768]{0:T(1024)} %get-tuple-element.754, s32[768]{0:T(1024)} %get-tuple-element.752, s32[9216]{0:T(1024)S(1)} %get-tuple-element.753, s32[768]{0:T(1024)} %get-tuple-element.750, s32[9216]{0:T(1024)S(1)} %get-tuple-element.751, s32[768]{0:T(1024)} %get-tuple-element.747, ...), kind=kOutput, calls=%fused_computation.4.clone.1 | convolution fusion | flops 1889795328 | bytes 31007744 | tf_op jit(solution)/shard_map/while/body/eval_jaxpr/qd,kd->qk/dot_general | solution.py:49
  212.9 24.7 %fusion.127 = f32[768]{0:T(1024)S(1)} fusion(f32[768,9216]{1,0:T(8,128)} %get-tuple-element.625, f32[768]{0:T(1024)S(1)} %max.26, s32[768]{0:T(1024)} %get-tuple-element.754, s32[768]{0:T(1024)} %get-tuple-element.752, s32[9216]{0:T(1024)S(1)} %get-tuple-element.753, s32[768]{0:T(1024)} %get-tuple-element.750, s32[9216]{0:T(1024)S(1)} %get-tuple-element.751, ...), kind=kLoop, calls=%fused_computation.6.clone.1 | loop fusion | flops 84933888 | bytes 28449792 | tf_op jit(solution)/shard_map/while/body/eval_jaxpr/reduce_sum | solution.py:59
  238.6 20.4 %fusion.129 = bf16[768,384]{1,0:T(8,128)(2,1)} fusion(bf16[768,384]{1,0:T(8,128)(2,1)} %get-tuple-element.722, s32[]{:T(128)S(6)} %select_n.177, f32[768,128]{1,0:T(8,128)S(1)} %fusion.126, bf16[9216,384]{1,0:T(8,128)(2,1)} %get-tuple-element.745, f32[768,9216]{1,0:T(8,128)S(1)} %copy-done.1, f32[768]{0:T(1024)} %copy-done.11, f32[768]{0:T(1024)} %add.240, ...), kind=kOutput, calls=%fused_computation.16.clone.1 | convolution fusion | flops 1897168896 | bytes 31406080 | tf_op jit(solution)/shard_map/while/body/eval_jaxpr/dot_general | solution.py:60
  259.0 22.9 %select_reduce_fusion.4 = (f32[768]{0:T(1024)S(1)}, f32[768,9216]{1,0:T(8,128)}) fusion(s32[768]{0:T(1024)} %get-tuple-element.754, s32[768]{0:T(1024)} %get-tuple-element.752, s32[9216]{0:T(1024)S(1)} %get-tuple-element.753, s32[768]{0:T(1024)} %get-tuple-element.750, s32[9216]{0:T(1024)S(1)} %get-tuple-element.751, s32[768]{0:T(1024)} %get-tuple-element.747, ...), kind=kOutput, calls=%fused_computation.4.clone.1 | convolution fusion | flops 1889795328 | bytes 31007744 | tf_op jit(solution)/shard_map/while/body/eval_jaxpr/qd,kd->qk/dot_general | solution.py:49
  283.2 24.7 %fusion.127 = f32[768]{0:T(1024)S(1)} fusion(f32[768,9216]{1,0:T(8,128)} %get-tuple-element.625, f32[768]{0:T(1024)S(1)} %max.26, s32[768]{0:T(1024)} %get-tuple-element.754, s32[768]{0:T(1024)} %get-tuple-element.752, s32[9216]{0:T(1024)S(1)} %get-tuple-element.753, s32[768]{0:T(1024)} %get-tuple-element.750, s32[9216]{0:T(1024)S(1)} %get-tuple-element.751, ...), kind=kLoop, calls=%fused_computation.6.clone.1 | loop fusion | flops 84933888 | bytes 28449792 | tf_op jit(solution)/shard_map/while/body/eval_jaxpr/reduce_sum | solution.py:59
  308.9 20.4 %fusion.129 = bf16[768,384]{1,0:T(8,128)(2,1)} fusion(bf16[768,384]{1,0:T(8,128)(2,1)} %get-tuple-element.722, s32[]{:T(128)S(6)} %select_n.177, f32[768,128]{1,0:T(8,128)S(1)} %fusion.126, bf16[9216,384]{1,0:T(8,128)(2,1)} %get-tuple-element.745, f32[768,9216]{1,0:T(8,128)S(1)} %copy-done.1, f32[768]{0:T(1024)} %copy-done.11, f32[768]{0:T(1024)} %add.240, ...), kind=kOutput, calls=%fused_computation.16.clone.1 | convolution fusion | flops 1897168896 | bytes 31406080 | tf_op jit(solution)/shard_map/while/body/eval_jaxpr/dot_general | solution.py:60
  347.3 207.6 %while.29 = (s32[]{:T(128)}, bf16[768,384]{1,0:T(8,128)(2,1)}, bf16[768,384]{1,0:T(8,128)(2,1)S(1)}, bf16[9216,384]{1,0:T(8,128)(2,1)}, bf16[256,384]{1,0:T(8,12...) while((s32[]{:T(128)}, bf16[768,384]{1,0:T(8,128)(2,1)}, ...), condition=%wide.region_11.12_spmd.clone, body=%wide.region_6.11_spmd.clone.sunk | while | flops 3973741056 | bytes 207419824 | solution.py:69
  347.4 22.5 %select_reduce_fusion.5 = (f32[768]{0:T(1024)S(1)}, f32[768,9216]{1,0:T(8,128)}) fusion(s32[768]{0:T(1024)} %get-tuple-element.697, s32[768]{0:T(1024)} %get-tuple-element.695, s32[9216]{0:T(1024)S(1)} %get-tuple-element.696, s32[768]{0:T(1024)} %get-tuple-element.693, s32[9216]{0:T(1024)S(1)} %get-tuple-element.694, s32[768]{0:T(1024)} %get-tuple-element.690, ...), kind=kOutput, calls=%fused_computation.34.clone.1 | convolution fusion | flops 1889795328 | bytes 31007744 | tf_op jit(solution)/shard_map/while/body/eval_jaxpr/qd,kd->qk/dot_general | solution.py:49
  370.3 24.9 %fusion.136 = f32[768]{0:T(1024)S(1)} fusion(f32[768,9216]{1,0:T(8,128)} %get-tuple-element.644, f32[768]{0:T(1024)S(1)} %max.27, s32[768]{0:T(1024)S(1)} %copy-done.16, s32[768]{0:T(1024)} %get-tuple-element.695, s32[9216]{0:T(1024)S(1)} %get-tuple-element.696, s32[768]{0:T(1024)S(1)} %copy-done.15, s32[9216]{0:T(1024)S(1)} %get-tuple-element.694, ...), kind=kLoop, calls=%fused_computation.36.clone.1 | loop fusion | flops 84933888 | bytes 28449792 | tf_op jit(solution)/shard_map/while/body/eval_jaxpr/reduce_sum | solution.py:59
  396.1 20.3 %fusion.138 = bf16[768,384]{1,0:T(8,128)(2,1)} fusion(bf16[768,384]{1,0:T(8,128)(2,1)} %get-tuple-element.665, s32[]{:T(128)S(6)} %select_n.181, f32[768,128]{1,0:T(8,128)S(1)} %fusion.135, bf16[9216,384]{1,0:T(8,128)(2,1)} %get-tuple-element.688, f32[768,9216]{1,0:T(8,128)S(1)} %copy-done.2, f32[768]{0:T(1024)} %copy-done.12, f32[768]{0:T(1024)} %add.244, ...), kind=kOutput, calls=%fused_computation.46.clone.1 | convolution fusion | flops 1897168896 | bytes 31406080 | tf_op jit(solution)/shard_map/while/body/eval_jaxpr/dot_general | solution.py:60
  416.5 22.5 %select_reduce_fusion.5 = (f32[768]{0:T(1024)S(1)}, f32[768,9216]{1,0:T(8,128)}) fusion(s32[768]{0:T(1024)} %get-tuple-element.697, s32[768]{0:T(1024)} %get-tuple-element.695, s32[9216]{0:T(1024)S(1)} %get-tuple-element.696, s32[768]{0:T(1024)} %get-tuple-element.693, s32[9216]{0:T(1024)S(1)} %get-tuple-element.694, s32[768]{0:T(1024)} %get-tuple-element.690, ...), kind=kOutput, calls=%fused_computation.34.clone.1 | convolution fusion | flops 1889795328 | bytes 31007744 | tf_op jit(solution)/shard_map/while/body/eval_jaxpr/qd,kd->qk/dot_general | solution.py:49
  439.5 24.9 %fusion.136 = f32[768]{0:T(1024)S(1)} fusion(f32[768,9216]{1,0:T(8,128)} %get-tuple-element.644, f32[768]{0:T(1024)S(1)} %max.27, s32[768]{0:T(1024)S(1)} %copy-done.16, s32[768]{0:T(1024)} %get-tuple-element.695, s32[9216]{0:T(1024)S(1)} %get-tuple-element.696, s32[768]{0:T(1024)S(1)} %copy-done.15, s32[9216]{0:T(1024)S(1)} %get-tuple-element.694, ...), kind=kLoop, calls=%fused_computation.36.clone.1 | loop fusion | flops 84933888 | bytes 28449792 | tf_op jit(solution)/shard_map/while/body/eval_jaxpr/reduce_sum | solution.py:59
  465.3 20.3 %fusion.138 = bf16[768,384]{1,0:T(8,128)(2,1)} fusion(bf16[768,384]{1,0:T(8,128)(2,1)} %get-tuple-element.665, s32[]{:T(128)S(6)} %select_n.181, f32[768,128]{1,0:T(8,128)S(1)} %fusion.135, bf16[9216,384]{1,0:T(8,128)(2,1)} %get-tuple-element.688, f32[768,9216]{1,0:T(8,128)S(1)} %copy-done.2, f32[768]{0:T(1024)} %copy-done.12, f32[768]{0:T(1024)} %add.244, ...), kind=kOutput, calls=%fused_computation.46.clone.1 | convolution fusion | flops 1897168896 | bytes 31406080 | tf_op jit(solution)/shard_map/while/body/eval_jaxpr/dot_general | solution.py:60
  485.6 22.5 %select_reduce_fusion.5 = (f32[768]{0:T(1024)S(1)}, f32[768,9216]{1,0:T(8,128)}) fusion(s32[768]{0:T(1024)} %get-tuple-element.697, s32[768]{0:T(1024)} %get-tuple-element.695, s32[9216]{0:T(1024)S(1)} %get-tuple-element.696, s32[768]{0:T(1024)} %get-tuple-element.693, s32[9216]{0:T(1024)S(1)} %get-tuple-element.694, s32[768]{0:T(1024)} %get-tuple-element.690, ...), kind=kOutput, calls=%fused_computation.34.clone.1 | convolution fusion | flops 1889795328 | bytes 31007744 | tf_op jit(solution)/shard_map/while/body/eval_jaxpr/qd,kd->qk/dot_general | solution.py:49
  508.6 24.9 %fusion.136 = f32[768]{0:T(1024)S(1)} fusion(f32[768,9216]{1,0:T(8,128)} %get-tuple-element.644, f32[768]{0:T(1024)S(1)} %max.27, s32[768]{0:T(1024)S(1)} %copy-done.16, s32[768]{0:T(1024)} %get-tuple-element.695, s32[9216]{0:T(1024)S(1)} %get-tuple-element.696, s32[768]{0:T(1024)S(1)} %copy-done.15, s32[9216]{0:T(1024)S(1)} %get-tuple-element.694, ...), kind=kLoop, calls=%fused_computation.36.clone.1 | loop fusion | flops 84933888 | bytes 28449792 | tf_op jit(solution)/shard_map/while/body/eval_jaxpr/reduce_sum | solution.py:59
  534.4 20.3 %fusion.138 = bf16[768,384]{1,0:T(8,128)(2,1)} fusion(bf16[768,384]{1,0:T(8,128)(2,1)} %get-tuple-element.665, s32[]{:T(128)S(6)} %select_n.181, f32[768,128]{1,0:T(8,128)S(1)} %fusion.135, bf16[9216,384]{1,0:T(8,128)(2,1)} %get-tuple-element.688, f32[768,9216]{1,0:T(8,128)S(1)} %copy-done.2, f32[768]{0:T(1024)} %copy-done.12, f32[768]{0:T(1024)} %add.244, ...), kind=kOutput, calls=%fused_computation.46.clone.1 | convolution fusion | flops 1897168896 | bytes 31406080 | tf_op jit(solution)/shard_map/while/body/eval_jaxpr/dot_general | solution.py:60
  563.9 9.6 %copy.9 = bf16[192,8,8,384]{3,2,1,0:T(8,128)(2,1)} copy(bf16[192,8,8,384]{3,1,2,0:T(8,128)(2,1)} %bitcast.25) | data formatting | bytes 18874368
  582.7 92.5 %all_to_all.5 = bf16[8,12,8,16,384]{4,3,2,1,0:T(8,128)(2,1)} all-to-all(bf16[8,12,8,16,384]{4,3,2,1,0:T(8,128)(2,1)} %bitcast.18), channel_id=1, replica_groups=mesh['ha'=4,'wa'=4,'hd'=8] {'hd'}, dimensions={0} | all-to-all | bytes 18874368 | tf_op jit(solution)/shard_map/all_to_all | solution.py:33
  (161 shorter events, 115.0 us)
Async XLA Ops:
  0.0 556.3 %copy-start = (bf16[384,3072]{1,0:T(8,128)(2,1)S(1)}, bf16[384,3072]{1,0:T(8,128)(2,1)}, u32[]{:S(2)}) copy-start(bf16[384,3072]{1,0:T(8,128)(2,1)} %param.17) | copy-start | bytes 7077892
  2.0 52.7 %copy-start.17 = (s32[3,2,1,2]{0,3,2,1:T(2,128)S(1)}, s32[3,2,1,2]{0,3,2,1:T(2,128)}, u32[]{:S(2)}) copy-start(s32[3,2,1,2]{0,3,2,1:T(2,128)} %param.16) | copy-start | bytes 148
  2.1 102.8 %copy-start.3 = (bf16[12,8,16,384]{3,2,1,0:T(8,128)(2,1)S(1)}, bf16[12,8,16,384]{3,2,1,0:T(8,128)(2,1)}, u32[]{:S(2)}) copy-start(bf16[12,8,16,384]{3,2,1,0:T(8,128)(2,1)} %param.13) | copy-start | bytes 3538948
  2.1 30.0 %collective-permute-start = (bf16[2,12,8,16,384]{4,3,2,1,0:T(8,128)(2,1)S(1)}, bf16[2,12,8,16,384]{4,3,2,1,0:T(8,128)(2,1)S(1)}, u32[]{:S(2)}, u32[]{:S(2)}) collective-permute-start(bf16[2,12,8,16,384]{4,3,2,1,0:T(8,128)(2,1)S(1)} %pad_maximum_fusion.2), channel_id=1, source_target_pairs={{0,32},{32,64},{64,96},{1,33},{33,65},{65,97},{2,34},{34,66},{66,9... | collective-permute-start | bytes 7077896 | tf_op jit(solution)/shard_map/ppermute | solution.py:17
  6.3 30.6 %collective-permute-start.1 = (bf16[2,12,8,16,384]{4,3,2,1,0:T(8,128)(2,1)S(1)}, bf16[2,12,8,16,384]{4,3,2,1,0:T(8,128)(2,1)S(1)}, u32[]{:S(2)}, u32[]{:S(2)}) collective-permute-start(bf16[2,12,8,16,384]{4,3,2,1,0:T(8,128)(2,1)S(1)} %pad_maximum_fusion.2), channel_id=1, source_target_pairs={{32,0},{64,32},{96,64},{33,1},{65,33},{97,65},{34,2},{66,34},{98,6... | collective-permute-start | bytes 7077896 | tf_op jit(solution)/shard_map/ppermute | solution.py:20
  44.8 56.8 %collective-permute-start.2 = (bf16[2,12,24,8,384]{4,3,2,1,0:T(8,128)(2,1)}, bf16[2,12,24,8,384]{4,3,2,1,0:T(8,128)(2,1)}, u32[]{:S(2)}, u32[]{:S(2)}) collective-permute-start(bf16[2,12,24,8,384]{4,3,2,1,0:T(8,128)(2,1)} %get-tuple-element.441), channel_id=1, source_target_pairs={{0,8},{8,16},{16,24},{1,9},{9,17},{17,25},{2,10},{10,18},{18,26},{... | collective-permute-start | bytes 10616840 | tf_op jit(solution)/shard_map/ppermute | solution.py:17
  47.8 57.1 %collective-permute-start.3 = (bf16[2,12,24,8,384]{4,3,2,1,0:T(8,128)(2,1)}, bf16[2,12,24,8,384]{4,3,2,1,0:T(8,128)(2,1)}, u32[]{:S(2)}, u32[]{:S(2)}) collective-permute-start(bf16[2,12,24,8,384]{4,3,2,1,0:T(8,128)(2,1)} %get-tuple-element.442), channel_id=1, source_target_pairs={{8,0},{16,8},{24,16},{9,1},{17,9},{25,17},{10,2},{18,10},{26,18},{... | collective-permute-start | bytes 10616840 | tf_op jit(solution)/shard_map/ppermute | solution.py:20
  117.9 229.4 %copy-start.8 = (bf16[6,8,16,384]{3,2,1,0:T(8,128)(2,1)S(1)}, bf16[6,8,16,384]{3,2,1,0:T(8,128)(2,1)}, u32[]{:S(2)}) copy-start(bf16[6,8,16,384]{3,2,1,0:T(8,128)(2,1)} %get-tuple-element.444) | copy-start | bytes 1769476
  142.4 25.5 %copy-start.11 = (f32[768]{0:T(1024)}, f32[768]{0:T(1024)S(1)}, u32[]{:S(2)}) copy-start(f32[768]{0:T(1024)S(1)} %max.26) | copy-start | bytes 9220 | tf_op jit(solution)/shard_map/while
  142.6 25.7 %copy-start.1 = (f32[768,9216]{1,0:T(8,128)S(1)}, f32[768,9216]{1,0:T(8,128)}, u32[]{:S(2)}) copy-start(f32[768,9216]{1,0:T(8,128)} %get-tuple-element.625) | copy-start | bytes 84934656 | tf_op jit(solution)/shard_map/while
  212.8 25.5 %copy-start.11 = (f32[768]{0:T(1024)}, f32[768]{0:T(1024)S(1)}, u32[]{:S(2)}) copy-start(f32[768]{0:T(1024)S(1)} %max.26) | copy-start | bytes 9220 | tf_op jit(solution)/shard_map/while
  212.9 25.7 %copy-start.1 = (f32[768,9216]{1,0:T(8,128)S(1)}, f32[768,9216]{1,0:T(8,128)}, u32[]{:S(2)}) copy-start(f32[768,9216]{1,0:T(8,128)} %get-tuple-element.625) | copy-start | bytes 84934656 | tf_op jit(solution)/shard_map/while
  283.1 25.5 %copy-start.11 = (f32[768]{0:T(1024)}, f32[768]{0:T(1024)S(1)}, u32[]{:S(2)}) copy-start(f32[768]{0:T(1024)S(1)} %max.26) | copy-start | bytes 9220 | tf_op jit(solution)/shard_map/while
  283.2 25.7 %copy-start.1 = (f32[768,9216]{1,0:T(8,128)S(1)}, f32[768,9216]{1,0:T(8,128)}, u32[]{:S(2)}) copy-start(f32[768,9216]{1,0:T(8,128)} %get-tuple-element.625) | copy-start | bytes 84934656 | tf_op jit(solution)/shard_map/while
  370.1 25.7 %copy-start.12 = (f32[768]{0:T(1024)}, f32[768]{0:T(1024)S(1)}, u32[]{:S(2)}) copy-start(f32[768]{0:T(1024)S(1)} %max.27) | copy-start | bytes 9220 | tf_op jit(solution)/shard_map/while
  370.3 25.8 %copy-start.2 = (f32[768,9216]{1,0:T(8,128)S(1)}, f32[768,9216]{1,0:T(8,128)}, u32[]{:S(2)}) copy-start(f32[768,9216]{1,0:T(8,128)} %get-tuple-element.644) | copy-start | bytes 84934656 | tf_op jit(solution)/shard_map/while
  416.5 23.0 %copy-start.16 = (s32[768]{0:T(1024)S(1)}, s32[768]{0:T(1024)}, u32[]{:S(2)}) copy-start(s32[768]{0:T(1024)} %get-tuple-element.697) | copy-start | bytes 9220 | tf_op jit(solution)/shard_map/while
  439.3 25.7 %copy-start.12 = (f32[768]{0:T(1024)}, f32[768]{0:T(1024)S(1)}, u32[]{:S(2)}) copy-start(f32[768]{0:T(1024)S(1)} %max.27) | copy-start | bytes 9220 | tf_op jit(solution)/shard_map/while
  439.4 25.8 %copy-start.2 = (f32[768,9216]{1,0:T(8,128)S(1)}, f32[768,9216]{1,0:T(8,128)}, u32[]{:S(2)}) copy-start(f32[768,9216]{1,0:T(8,128)} %get-tuple-element.644) | copy-start | bytes 84934656 | tf_op jit(solution)/shard_map/while
  485.6 23.0 %copy-start.14 = (s32[768]{0:T(1024)S(1)}, s32[768]{0:T(1024)}, u32[]{:S(2)}) copy-start(s32[768]{0:T(1024)} %get-tuple-element.690) | copy-start | bytes 9220 | tf_op jit(solution)/shard_map/while
  485.6 23.0 %copy-start.15 = (s32[768]{0:T(1024)S(1)}, s32[768]{0:T(1024)}, u32[]{:S(2)}) copy-start(s32[768]{0:T(1024)} %get-tuple-element.693) | copy-start | bytes 9220 | tf_op jit(solution)/shard_map/while
  485.6 23.0 %copy-start.16 = (s32[768]{0:T(1024)S(1)}, s32[768]{0:T(1024)}, u32[]{:S(2)}) copy-start(s32[768]{0:T(1024)} %get-tuple-element.697) | copy-start | bytes 9220 | tf_op jit(solution)/shard_map/while
  508.4 25.7 %copy-start.12 = (f32[768]{0:T(1024)}, f32[768]{0:T(1024)S(1)}, u32[]{:S(2)}) copy-start(f32[768]{0:T(1024)S(1)} %max.27) | copy-start | bytes 9220 | tf_op jit(solution)/shard_map/while
  508.6 25.8 %copy-start.2 = (f32[768,9216]{1,0:T(8,128)S(1)}, f32[768,9216]{1,0:T(8,128)}, u32[]{:S(2)}) copy-start(f32[768,9216]{1,0:T(8,128)} %get-tuple-element.644) | copy-start | bytes 84934656 | tf_op jit(solution)/shard_map/while
  (14 other events, 230.6 us)
where the time goes:
time: 691 us; the launch traced here: 682 us
  matrix products  272 us (39%)
  other arithmetic  174 us (25%)
  blocking collectives  92.5 us (13%)
  local copies, waits for them, and re-layouts  66.6 us (10%)
  waiting for transfers between devices  47.3 us (7%)
  loops' own time  18 us (3%)
  starting transfers between devices  11.4 us (2%)
    reduce_sum x12, other arithmetic, one_head(): row_total = jnp.sum(weights, axis=1) + jnp.sum(text_weights, axis=1)  150 us
    dot_general x6, matrix products, one_head(): jnp.einsum('qd,kd->qk', q_head, k_head, preferred_element_type=jnp.float32)  136 us
    dot_general x6, matrix products, one_head(): jnp.dot(weights.astype(jnp.bfloat16), v_head, preferred_element_type=jnp....  122 us
    all_to_all x1, blocking collectives, summed_on_arrival(): lax.all_to_all(blocks, axis, split_axis=0, concat_axis=0, tiled=True)  92.5 us
    ppermute x2, waiting for transfers between devices, extended(): lax.ppermute(lax.slice_in_dim(block, block.shape[dim] - width, None, axis...  39.3 us
    another operation x2, loops' own time, attend(): lax.fori_loop(0, head_count, one_head, jnp.zeros(q_block.shape, jnp.bfloa...  18 us
  transfers between devices with their start and end apart: 4, of which 4 were waited for; matrix products, arithmetic and copies ran while one was open for 5% of the time, Pallas kernels for 0%

commit v1 on v0

v1 whole, which is shorter than its diff:
```python
import functools

import jax
import jax.numpy as jnp
from jax import lax
from jax.experimental import pallas as pl
from jax.experimental.pallas import tpu as pltpu
from jax.sharding import PartitionSpec as P

HEAD = 128
TILE_T = 6
TILE_H = 8
TILE_W = 8
FACTOR = 1.4426950408889634 * HEAD ** (-0.5)
FAR = 1e30
SUB = 256


def summed_on_arrival(value, axis, dim):
    size = lax.axis_size(axis)
    shape = value.shape
    blocks = value.reshape(*shape[:dim], size, shape[dim] // size, *shape[dim + 1 :])
    blocks = jnp.moveaxis(blocks, dim, 0)
    arrived = lax.all_to_all(blocks, axis, split_axis=0, concat_axis=0, tiled=True)
    return arrived.astype(jnp.float32).sum(axis=0)


def tiled(block):
    frames, height, across, channels = block.shape
    cols = across // TILE_W
    heads = channels // HEAD
    cut = block.reshape(frames, height, cols, TILE_W, heads, HEAD)
    return cut.transpose(4, 2, 0, 1, 3, 5).reshape(heads, cols, -1, HEAD)


def untiled(tiles, frames, height):
    cols, _, channels = tiles.shape
    cut = tiles.reshape(cols, frames, height, TILE_W, channels)
    return cut.transpose(1, 2, 0, 3, 4).reshape(frames, height, cols * TILE_W, channels)


def fold_chunk(q, k, v, pens, m_ref, l_ref, acc_ref, first=False):
    count = len(pens)
    keys = k.shape[0] // count
    for start in range(0, q.shape[0], SUB):
        at = slice(start, start + SUB)
        s = FACTOR * lax.dot_general(
            k, q[at], (((1,), (1,)), ((), ())), preferred_element_type=jnp.float32
        )
        parts = [s[i * keys : (i + 1) * keys] for i in range(count)]
        tops = [jnp.max(part, axis=0, keepdims=True) for part in parts]
        rows = [None if pen is None else pen[:, at] for pen in pens]
        tops = [top if row is None else top - row for top, row in zip(tops, rows)]
        m_new = functools.reduce(jnp.maximum, tops)
        if not first:
            m_old = m_ref[:, at]
            m_new = jnp.maximum(m_new, m_old)
        weights = [
            jnp.exp2(part - (m_new if row is None else m_new + row))
            for part, row in zip(parts, rows)
        ]
        total = functools.reduce(
            jnp.add, [jnp.sum(weight, axis=0, keepdims=True) for weight in weights]
        )
        low = [weight.astype(jnp.bfloat16) for weight in weights]
        low = low[0] if count == 1 else jnp.concatenate(low, axis=0)
        add = lax.dot_general(
            v, low, (((0,), (0,)), ((), ())), preferred_element_type=jnp.float32
        )
        if first:
            l_ref[:, at] = total
            acc_ref[:, at] = add
        else:
            shrink = jnp.exp2(m_old - m_new)
            l_ref[:, at] = l_ref[:, at] * shrink + total
            acc_ref[:, at] = acc_ref[:, at] * shrink + add
        m_ref[:, at] = m_new


def attend_kernel(radius, q_ref, kv_ref, tk_ref, tv_ref, out_ref, m_ref, l_ref, acc_ref):
    col = pl.program_id(1)
    ha, wa = lax.axis_index("ha"), lax.axis_index("wa")
    rows, cols = lax.axis_size("ha"), 2 * lax.axis_size("wa")
    q = q_ref[0, 0]
    fold_chunk(q, tk_ref[...], tv_ref[...], [None], m_ref, l_ref, acc_ref, first=True)
    late = lax.broadcasted_iota(jnp.int32, (1, q.shape[0]), 1) >= q.shape[0] // 2

    def visit(i, carry):
        row, gap = i // 3, i % 3
        key_row, key_col = ha + row - 1, 2 * wa + col + gap - 1
        there = (key_row >= 0) & (key_row < rows) & (key_col >= 0) & (key_col < cols)
        seen = []
        for t in range(2):
            seen.append(
                there
                & (jnp.abs(row - 1) <= radius[2 + t, col])
                & (jnp.abs(gap - 1) <= radius[4 + t, col])
            )

        @pl.when(seen[0] | seen[1])
        def _():
            pens = []
            for kt in range(2):
                pen = []
                for qt in range(2):
                    ok = seen[qt] & (abs(qt - kt) <= radius[qt, col])
                    pen.append(jnp.where(ok, 0.0, FAR))
                pens.append(jnp.where(late, pen[1], pen[0]))
            kv = kv_ref.at[row, col + gap, 0]
            fold_chunk(q, kv[0], kv[1], pens, m_ref, l_ref, acc_ref)

        return carry

    lax.fori_loop(0, 9, visit, 0)
    out_ref[0] = (acc_ref[...] / l_ref[...]).T.astype(out_ref.dtype)


def attend(radius, q, kv, text_keys, text_values):
    heads, cols, tokens, _ = q.shape
    grid = (heads, cols)
    return pl.pallas_call(
        attend_kernel,
        grid_spec=pltpu.PrefetchScalarGridSpec(
            num_scalar_prefetch=1,
            grid=grid,
            in_specs=[
                pl.BlockSpec((1, 1, tokens, HEAD), lambda h, c, r: (h, c, 0, 0)),
                pl.BlockSpec((3, 4, 1, 2, tokens, HEAD), lambda h, c, r: (0, 0, h, 0, 0, 0)),
                pl.BlockSpec((text_keys.shape[0], HEAD), lambda h, c, r: (0, h)),
                pl.BlockSpec((text_keys.shape[0], HEAD), lambda h, c, r: (0, h)),
            ],
            out_specs=pl.BlockSpec((1, tokens, HEAD), lambda h, c, r: (c, 0, h)),
            scratch_shapes=[
                pltpu.VMEM((1, tokens), jnp.float32),
                pltpu.VMEM((1, tokens), jnp.float32),
                pltpu.VMEM((HEAD, tokens), jnp.float32),
            ],
        ),
        out_shape=jax.ShapeDtypeStruct((cols, tokens, heads * HEAD), jnp.bfloat16),
        compiler_params=pltpu.CompilerParams(vmem_limit_bytes=56 * 1024 * 1024),
        cost_estimate=pl.CostEstimate(
            flops=20_000_000_000, bytes_accessed=18_000_000, transcendentals=30_000_000
        ),
        name="attend",
    )(radius, q, kv, text_keys, text_values)


def shifts(block, axis):
    count = lax.axis_size(axis)
    forward = [(i, i + 1) for i in range(count - 1)]
    backward = [(i + 1, i) for i in range(count - 1)]
    return lax.ppermute(block[0], axis, forward), lax.ppermute(block[1], axis, backward)


def shards(queries, video_keys, video_values, text_keys, text_values, tile_radius, out_weight):
    n_frames, height, across, channels = queries.shape
    q = tiled(queries)
    kv = jnp.stack([tiled(video_keys), tiled(video_values)], axis=2)
    kv = jnp.moveaxis(kv, 1, 0)
    left, right = shifts((kv[1:], kv[:1]), "wa")
    row = jnp.concatenate([left, kv, right], axis=0)
    above, below = shifts((row, row), "ha")
    window = jnp.stack([above, row, below])
    radius = tile_radius[:, :, 0, :].reshape(6, -1)
    mixture = attend(radius, q, window, text_keys, text_values)
    portion = jnp.dot(mixture.reshape(-1, channels), out_weight, preferred_element_type=jnp.float32)
    portion = portion.astype(jnp.bfloat16).reshape(across // TILE_W, -1, out_weight.shape[1])
    summed = summed_on_arrival(portion, "hd", 2).astype(jnp.bfloat16)
    return untiled(summed, n_frames, height)


def solution(mesh):
    placed = (
        P(None, "ha", "wa", "hd"),
        P(None, "ha", "wa", "hd"),
        P(None, "ha", "wa", "hd"),
        P(None, "hd"),
        P(None, "hd"),
        P(None, None, "ha", "wa"),
        P("hd", None),
    )
    return jax.shard_map(
        shards, mesh=mesh, in_specs=placed, out_specs=P(None, "ha", "wa", "hd"), check_vma=False
    )
```

time: 691 us -> 317 us (0.46); the launches traced: 682 us -> 317 us
  matrix products: 272 us -> 8.95 us
  other arithmetic: 174 us -> 22.4 us
  Pallas kernels: 0 us -> 107 us
  local copies, waits for them, and re-layouts: 66.6 us -> 24 us
  waiting for transfers between devices: 47.3 us -> 77.8 us
  blocking collectives: 92.5 us -> 63.9 us
  loops' own time: 18 us -> 0 us
    dot_general x24 -> x0, matrix products: 265 us -> none  [the longest x6 136 us: one_head(): jnp.einsum('qd,kd->qk', q_head, k_head, preferred_element_type=jnp.float32)]
    reduce_sum x12 -> x0, other arithmetic: 150 us -> none  [one_head(): row_total = jnp.sum(weights, axis=1) + jnp.sum(text_weights, axis=1)]
    pallas_call x0 -> x1, Pallas kernels: none -> 107 us  [attend(): pl.pallas_call(attend_kernel, grid_spec=pltpu.PrefetchScalarGridSpec(num_...]
    ppermute x4, waiting for transfers between devices: 47.3 us -> 77.8 us  [the longest x2 70.6 us: shifts(): lax.ppermute(block[0], axis, forward)]
    all_to_all x1, blocking collectives: 92.5 us -> 63.9 us  [summed_on_arrival(): lax.all_to_all(blocks, axis, split_axis=0, concat_axis=0, tiled=True)]
    broadcast_in_dim x30 -> x0, local copies, waits for them, and re-layouts: 23.4 us -> none  [the longest x12 12.1 us: shards(): jnp.broadcast_to(radii_row[:, None, None, :], (3, TILE_T, TILE_H, across))]
    another operation x2 -> x0, loops' own time: 18 us -> none  [attend(): lax.fori_loop(0, head_count, one_head, jnp.zeros(q_block.shape, jnp.bfloa...]
    another operation x1 -> x2, other arithmetic: 2.04 us -> 16.8 us  [shards(): window = jnp.stack([above, row, below])]
  transfers between devices with their start and end apart: 4 -> 4, of which waited for: 4 -> 4; matrix products, arithmetic and copies ran while one was open for 5% -> 1% of each run, Pallas kernels for 0% -> 0%
where the time goes in v1:
time: 317 us
  Pallas kernels  107 us (34%)
  waiting for transfers between devices  77.8 us (25%)
  blocking collectives  63.9 us (20%)
  local copies, waits for them, and re-layouts  24 us (8%)
  other arithmetic  22.4 us (7%)
  starting transfers between devices  12.8 us (4%)
  matrix products  8.95 us (3%)
    pallas_call x1, Pallas kernels, attend(): pl.pallas_call(attend_kernel, grid_spec=pltpu.PrefetchScalarGridSpec(num_...  107 us
    ppermute x2, waiting for transfers between devices, shifts(): lax.ppermute(block[0], axis, forward)  70.6 us
    all_to_all x1, blocking collectives, summed_on_arrival(): lax.all_to_all(blocks, axis, split_axis=0, concat_axis=0, tiled=True)  63.9 us
    another operation x2, other arithmetic, shards(): window = jnp.stack([above, row, below])  16.8 us
    unnamed x9, local copies, waits for them, and re-layouts  9.66 us
    dot_general x1, matrix products, shards(): jnp.dot(mixture.reshape(-1, channels), out_weight, preferred_element_type...  8.95 us
    another operation x1, local copies, waits for them, and re-layouts, summed_on_arrival(): value.reshape(*shape[:dim], size, shape[dim] // size, *shape[dim + 1:])  8.87 us
    ppermute x2, starting transfers between devices, shifts(): lax.ppermute(block[0], axis, forward)  8.27 us
  transfers between devices with their start and end apart: 4, of which 4 were waited for; matrix products, arithmetic and copies ran while one was open for 1% of the time, Pallas kernels for 0%

profile of v1, /device:TPU:17, one launch (start us, length us, event | category | flops | bytes accessed | tf_op | source)
XLA Modules:
  0.0 316.5 jit_solution(11451829367953648012)
XLA Ops:
  0.0 1.8 copy.26
  1.8 0.3 copy.27
  2.1 0.2 maximum_bitcast_fusion
  2.4 0.2 fusion.1
  2.5 2.9 collective-permute-start
  5.4 2.5 collective-permute-start.1
  8.0 23.3 %collective-permute-done = bf16[1,3,2,768,128]{4,3,2,1,0:T(8,128)(2,1)S(1)} collective-permute-done((bf16[1,3,2,768,128]{4,3,2,1,0:T(8,128)(2,1)S(1)}, bf16[1,3,2,768,128]{4,3,2,1,0:T(8,128)(2,1)S(1)}, u32[]{:S(2)}, u32[]{:S(2)}) %collective-permute-start) | collective-permute-done | bytes 1179680 | tf_op jit(solution)/shard_map/ppermute | solution.py:152
  31.3 2.8 collective-permute-done.1
  34.0 3.9 %fusion = (bf16[1,4,3,2,768,128]{5,4,3,2,1,0:T(8,128)(2,1)}, bf16[4,3,2,768,128]{4,3,2,1,0:T(8,128)(2,1)}) fusion(bf16[1,3,2,768,128]{4,3,2,1,0:T(8,128)(2,1)S(1)} %collective-permute-done.1, bf16[2,3,2,768,128]{4,3,2,1,0:T(8,128)(2,1)S(1)} %maximum_bitcast_fusion, bf16[1,3,2,768,128]{4,3,2,1,0:T(8,128)(2,1)S(1)} %collective-permute-done), kind=kLoop, calls=%fused_computation.6 | loop fusion | flops 4718592 | bytes 14155776 | tf_op jit(solution)/shard_map/stack | solution.py:163
  38.0 5.4 %collective-permute-start.2 = (bf16[4,3,2,768,128]{4,3,2,1,0:T(8,128)(2,1)}, bf16[4,3,2,768,128]{4,3,2,1,0:T(8,128)(2,1)}, u32[]{:S(2)}, u32[]{:S(2)}) collective-permute-start(bf16[4,3,2,768,128]{4,3,2,1,0:T(8,128)(2,1)} %get-tuple-element.6), channel_id=1, source_target_pairs={{0,32},{32,64},{64,96},{1,33},{33,65},{65,97},{2,34},{34,66},{66,9... | collective-permute-start | bytes 14155784 | tf_op jit(solution)/shard_map/ppermute | solution.py:152
  43.3 2.0 collective-permute-start.3
  45.4 1.4 copy.25
  46.7 0.1 copy.31
  46.8 0.6 reshape.28.radius
  47.4 47.3 %collective-permute-done.2 = bf16[4,3,2,768,128]{4,3,2,1,0:T(8,128)(2,1)} collective-permute-done((bf16[4,3,2,768,128]{4,3,2,1,0:T(8,128)(2,1)}, bf16[4,3,2,768,128]{4,3,2,1,0:T(8,128)(2,1)}, u32[]{:S(2)}, u32[]{:S(2)}) %collective-permute-start.2) | collective-permute-done | bytes 4718624 | tf_op jit(solution)/shard_map/ppermute | solution.py:152
  94.7 4.4 %collective-permute-done.3 = bf16[4,3,2,768,128]{4,3,2,1,0:T(8,128)(2,1)} collective-permute-done((bf16[4,3,2,768,128]{4,3,2,1,0:T(8,128)(2,1)}, bf16[4,3,2,768,128]{4,3,2,1,0:T(8,128)(2,1)}, u32[]{:S(2)}, u32[]{:S(2)}) %collective-permute-start.3) | collective-permute-done | bytes 4718624 | tf_op jit(solution)/shard_map/ppermute | solution.py:152
  99.1 12.9 %pad_maximum_fusion.kv_ref = bf16[3,4,3,2,768,128]{5,4,3,2,1,0:T(8,128)(2,1)} fusion(bf16[1,4,3,2,768,128]{5,4,3,2,1,0:T(8,128)(2,1)} %bitcast.12, bf16[1,4,3,2,768,128]{5,4,3,2,1,0:T(8,128)(2,1)} %get-tuple-element.5, bf16[1,4,3,2,768,128]{5,4,3,2,1,0:T(8,128)(2,1)} %bitcast.10), kind=kLoop, calls=%fused_computation | loop fusion | flops 14155776 | bytes 28311552 | tf_op jit(solution)/shard_map/stack | solution.py:163
  112.0 106.6 %attend.1 = bf16[2,768,384]{2,1,0:T(8,128)(2,1)} custom-call(s32[6,2]{1,0:T(8,128)} %reshape.28.radius, bf16[3,2,768,128]{3,2,1,0:T(8,128)(2,1)} %bitcast.44, bf16[3,4,3,2,768,128]{5,4,3,2,1,0:T(8,128)(2,1)} %pad_maximum_fusion.kv_ref, bf16[256,384]{1,0:T(8,128)(2,1)} %tk_ref.1, bf16[256,384]{1,0:T(8,128)(2,1)} %tv_ref.1), custom_call_target="tpu_custom_call" | custom-call | flops 20000000000 | bytes 18000000 | tf_op jit(solution)/shard_map/attend/pallas_call | solution.py:121
  218.6 9.0 %convolution_convert_fusion = bf16[1536,3072]{1,0:T(8,128)(2,1)} fusion(bf16[1536,384]{1,0:T(8,128)(2,1)} %bitcast.45, bf16[384,3072]{1,0:T(8,128)(2,1)S(1)} %copy-done), kind=kOutput, calls=%fused_computation.1 | convolution fusion | flops 3628597248 | bytes 12976128 | tf_op jit(solution)/shard_map/dot_general | solution.py:166
  227.6 9.6 %copy.33 = bf16[192,8,8,384]{3,2,1,0:T(8,128)(2,1)} copy(bf16[192,8,8,384]{3,1,2,0:T(8,128)(2,1)} %bitcast.37) | data formatting | bytes 18874368
  237.2 8.9 %copy.36 = bf16[2,768,8,384]{3,1,0,2:T(8,128)(2,1)} copy(bf16[2,768,8,384]{3,2,1,0:T(8,128)(2,1)} %bitcast.35) | data formatting | bytes 18874368 | tf_op jit(solution)/shard_map/reshape;reshape | solution.py:22
  246.1 63.9 %all_to_all.5 = bf16[8,2,768,384]{3,2,1,0:T(8,128)(2,1)} all-to-all(bf16[8,2,768,384]{3,2,1,0:T(8,128)(2,1)} %bitcast.36), channel_id=1, replica_groups=mesh['ha'=4,'wa'=4,'hd'=8] {'hd'}, dimensions={0} | all-to-all | bytes 18874368 | tf_op jit(solution)/shard_map/all_to_all | solution.py:24
  310.0 5.4 %reduce_sum.12 = bf16[2,768,384]{2,1,0:T(8,128)(2,1)S(1)} reduce(bf16[8,2,768,384]{3,2,1,0:T(8,128)(2,1)} %all_to_all.5, bf16[]{:T(256)} %constant.2.clone.1), dimensions={0}, to_apply=%region_0.0 | reduce | flops 4128768 | bytes 10616834 | tf_op jit(solution)/shard_map/reduce_sum | solution.py:25
  315.4 1.1 copy.37
  (8 shorter events, 0.0 us)
Async XLA Ops:
  0.0 218.6 %copy-start = (bf16[384,3072]{1,0:T(8,128)(2,1)S(1)}, bf16[384,3072]{1,0:T(8,128)(2,1)}, u32[]{:S(2)}) copy-start(bf16[384,3072]{1,0:T(8,128)(2,1)} %param.13) | copy-start | bytes 7077892
  0.0 1.8 copy-start.1
  2.5 28.7 %collective-permute-start = (bf16[1,3,2,768,128]{4,3,2,1,0:T(8,128)(2,1)S(1)}, bf16[1,3,2,768,128]{4,3,2,1,0:T(8,128)(2,1)S(1)}, u32[]{:S(2)}, u32[]{:S(2)}) collective-permute-start(bf16[1,3,2,768,128]{4,3,2,1,0:T(8,128)(2,1)S(1)} %get-tuple-element.7), channel_id=1, source_target_pairs={{0,8},{8,16},{16,24},{1,9},{9,17},{17,25},{2,10},{10,18},{18,26},{... | collective-permute-start | bytes 3538952 | tf_op jit(solution)/shard_map/ppermute | solution.py:152
  5.4 39.9 %copy-start.2 = (bf16[12,8,16,384]{3,2,1,0:T(8,128)(2,1)S(1)}, bf16[12,8,16,384]{3,2,1,0:T(8,128)(2,1)}, u32[]{:S(2)}) copy-start(bf16[12,8,16,384]{3,2,1,0:T(8,128)(2,1)} %param.7) | copy-start | bytes 3538948
  5.4 28.6 %collective-permute-start.1 = (bf16[1,3,2,768,128]{4,3,2,1,0:T(8,128)(2,1)S(1)}, bf16[1,3,2,768,128]{4,3,2,1,0:T(8,128)(2,1)S(1)}, u32[]{:S(2)}, u32[]{:S(2)}) collective-permute-start(bf16[1,3,2,768,128]{4,3,2,1,0:T(8,128)(2,1)S(1)} %get-tuple-element.8), channel_id=1, source_target_pairs={{8,0},{16,8},{24,16},{9,1},{17,9},{25,17},{10,2},{18,10},{26,18},{... | collective-permute-start | bytes 3538952 | tf_op jit(solution)/shard_map/ppermute | solution.py:152
  38.0 8.7 %copy-start.3 = (s32[3,2,1,2]{0,3,2,1:T(2,128)S(1)}, s32[3,2,1,2]{0,3,2,1:T(2,128)}, u32[]{:S(2)}) copy-start(s32[3,2,1,2]{0,3,2,1:T(2,128)} %param.12) | copy-start | bytes 148
  38.0 56.7 %collective-permute-start.2 = (bf16[4,3,2,768,128]{4,3,2,1,0:T(8,128)(2,1)}, bf16[4,3,2,768,128]{4,3,2,1,0:T(8,128)(2,1)}, u32[]{:S(2)}, u32[]{:S(2)}) collective-permute-start(bf16[4,3,2,768,128]{4,3,2,1,0:T(8,128)(2,1)} %get-tuple-element.6), channel_id=1, source_target_pairs={{0,32},{32,64},{64,96},{1,33},{33,65},{65,97},{2,34},{34,66},{66,9... | collective-permute-start | bytes 14155784 | tf_op jit(solution)/shard_map/ppermute | solution.py:152
  43.3 55.8 %collective-permute-start.3 = (bf16[4,3,2,768,128]{4,3,2,1,0:T(8,128)(2,1)}, bf16[4,3,2,768,128]{4,3,2,1,0:T(8,128)(2,1)}, u32[]{:S(2)}, u32[]{:S(2)}) collective-permute-start(bf16[4,3,2,768,128]{4,3,2,1,0:T(8,128)(2,1)} %get-tuple-element.6), channel_id=1, source_target_pairs={{32,0},{64,32},{96,64},{33,1},{65,33},{97,65},{34,2},{66,34},{98,6... | collective-permute-start | bytes 14155784 | tf_op jit(solution)/shard_map/ppermute | solution.py:152

commit v2 on v1

v2 whole, which is shorter than its diff:
```python
import functools

import jax
import jax.numpy as jnp
from jax import lax
from jax.experimental import pallas as pl
from jax.experimental.pallas import tpu as pltpu
from jax.sharding import PartitionSpec as P

HEAD = 128
TILE_W = 8
FACTOR = 1.4426950408889634 * HEAD ** (-0.5)
FAR = 1e30
SUB = 256
NX = 4
BF16 = jnp.bfloat16
F32 = jnp.float32
MESH = pl.DeviceIdType.MESH


def tiled(block):
    frames, height, across, channels = block.shape
    cols = across // TILE_W
    heads = channels // HEAD
    cut = block.reshape(frames, height, cols, TILE_W, heads, HEAD)
    return cut.transpose(4, 2, 0, 1, 3, 5).reshape(heads, cols, -1, HEAD)


def untiled(tiles, frames, height):
    cols, _, channels = tiles.shape
    cut = tiles.reshape(cols, frames, height, TILE_W, channels)
    return cut.transpose(1, 2, 0, 3, 4).reshape(frames, height, cols * TILE_W, channels)


def product(a, b, over_a, over_b):
    return lax.dot_general(a, b, (((over_a,), (over_b,)), ((), ())), preferred_element_type=F32)


def fold_chunk(q2, k, v, pens, m_ref, l_ref, acc_ref, s_ref, first=False):
    count = len(pens)
    keys = k.shape[0] // count
    k2 = jnp.concatenate([k, k], axis=1)
    for part, start in enumerate(range(0, q2.shape[0], SUB)):
        at = slice(start, start + SUB)
        s = product(k2, q2[at], 1, 1)
        held = s_ref.at[part]
        held[: k.shape[0]] = s
        tops = [
            jnp.max(s[i * keys : (i + 1) * keys], axis=0, keepdims=True) for i in range(count)
        ]
        rows = [None if pen is None else pen[:, at] for pen in pens]
        tops = [top if row is None else top - row for top, row in zip(tops, rows)]
        m_new = functools.reduce(jnp.maximum, tops)
        if not first:
            m_old = m_ref[:, at]
            m_new = jnp.maximum(m_new, m_old)
        weights = [
            jnp.exp2(held[i * keys : (i + 1) * keys] - (m_new if row is None else m_new + row))
            for i, row in enumerate(rows)
        ]
        total = functools.reduce(
            jnp.add, [jnp.sum(weight, axis=0, keepdims=True) for weight in weights]
        )
        low = [weight.astype(BF16) for weight in weights]
        low = low[0] if count == 1 else jnp.concatenate(low, axis=0)
        add = product(v, low, 0, 0)
        if first:
            l_ref[:, at] = total
            acc_ref[:, at] = add
        else:
            shrink = jnp.exp2(m_old - m_new)
            l_ref[:, at] = l_ref[:, at] * shrink + total
            acc_ref[:, at] = acc_ref[:, at] * shrink + add
        m_ref[:, at] = m_new


def layer_kernel(
    radius, q_ref, kv_ref, tk_ref, tv_ref, w_ref, out_ref,
    kvh, q2, m_ref, l_ref, acc_ref, s_ref, ag, wg, part, leave, arrive,
    row_s, row_r, par_s, par_r, z_s, z_r, parcol_s, parcol_r, zcol_s, zcol_r,
    w_s, w_r, wf_s, wf_r, wl, ag_s, ag_r, agf_s, agf_r, sum_s, sum_r,
):
    heads = q_ref.shape[0]
    tokens = q_ref.shape[2]
    width = heads * HEAD
    half = width // 2
    ha, wa, hd = lax.axis_index("ha"), lax.axis_index("wa"), lax.axis_index("hd")
    last = lax.axis_size("wa") - 1
    core = lax.rem(ha, 2)
    partner = ha + 1 - 2 * core
    inner = (ha == 1) | (ha == 2)
    peer = 3 - ha
    x = lax.rem(hd, NX)
    z = hd // NX
    near = 2 - 2 * core
    far = 2 * core
    has_left, has_right = wa > 0, wa < last

    def x_at(step):
        return z * NX + lax.rem(x + step, NX)

    def remote(src, dst, send, recv, device):
        return pltpu.make_async_remote_copy(
            src_ref=src, dst_ref=dst, send_sem=send, recv_sem=recv,
            device_id=device, device_id_type=MESH,
        )

    def row_copy(h, side):
        return remote(
            kv_ref.at[h, 1 - side], kvh.at[h, 1, 3 * side], row_s.at[h, side], row_r.at[h, side],
            {"wa": wa + 1 - 2 * side},
        )

    def par_copy(h):
        return remote(
            kv_ref.at[h], kvh.at[h, far, pl.ds(1, 2)], par_s.at[h], par_r.at[h], {"ha": partner}
        )

    def z_copy(h):
        return remote(
            kv_ref.at[h], kvh.at[h, near, pl.ds(1, 2)], z_s.at[h], z_r.at[h], {"ha": peer}
        )

    def parcol_copy(h, side):
        return remote(
            kvh.at[h, 1, 3 * side], kvh.at[h, far, 3 * side],
            parcol_s.at[h, side], parcol_r.at[h, side], {"ha": partner},
        )

    def zcol_copy(h, side):
        return remote(
            kvh.at[h, far, 2 - side], kvh.at[h, far, 3 * side],
            zcol_s.at[h, side], zcol_r.at[h, side], {"wa": wa + 1 - 2 * side},
        )

    def w_copy(step, zc):
        cols = pl.multiple_of((zc * NX + lax.rem(x + step, NX)) * width, HEAD)
        return remote(
            w_ref.at[pl.ds(core * half, half), pl.ds(cols, width)],
            wg.at[zc, pl.ds(x * width + core * half, half)],
            w_s.at[step - 1, zc], w_r.at[step - 1, zc], {"hd": x_at(step)},
        )

    def w_forward(step, zc):
        rows = pl.ds(lax.rem(x + NX - step, NX) * width + core * half, half)
        return remote(
            wg.at[zc, rows], wg.at[zc, rows],
            wf_s.at[step - 1, zc], wf_r.at[step - 1, zc], {"ha": partner},
        )

    def w_own(zc):
        cols = pl.multiple_of((zc * NX + x) * width, HEAD)
        return pltpu.make_async_copy(
            w_ref.at[:, pl.ds(cols, width)], wg.at[zc, pl.ds(x * width, width)], wl.at[zc]
        )

    def ag_copy(c, h, way):
        return remote(
            ag.at[c, x, h], ag.at[c, x, h], ag_s.at[c, h, way], ag_r.at[c, h, way],
            {"hd": x_at(1 + 2 * way)},
        )

    def ag_forward(c, h):
        block = ag.at[c, lax.rem(x + NX - 1 + 2 * c, NX), h]
        return remote(
            block, block, agf_s.at[c, h], agf_r.at[c, h], {"hd": x_at(1 + 2 * c)}
        )

    def sum_copy(c, b):
        at = pl.ds(b * SUB, SUB)
        return remote(
            leave.at[c, at], arrive.at[c, at], sum_s.at[c, b], sum_r.at[c, b],
            {"hd": lax.rem(hd + NX, 2 * NX)},
        )

    barrier = pltpu.get_barrier_semaphore()

    def greet(device):
        pl.semaphore_signal(barrier, inc=1, device_id=device, device_id_type=MESH)

    pl.when(has_left)(lambda: greet({"wa": wa - 1}))
    pl.when(has_right)(lambda: greet({"wa": wa + 1}))
    pl.when(inner)(lambda: greet({"ha": peer}))
    greet({"ha": partner})
    for step in range(1, NX):
        greet({"hd": x_at(step)})
    greet({"hd": lax.rem(hd + NX, 2 * NX)})
    pl.semaphore_wait(
        barrier,
        2 + NX - 1
        + has_left.astype(jnp.int32) + has_right.astype(jnp.int32) + inner.astype(jnp.int32),
    )

    def when_side(side, act):
        pl.when(has_right if side == 0 else has_left)(act)

    def when_from(side, act):
        pl.when(has_left if side == 0 else has_right)(act)

    def start_rows(h):
        for side in range(2):
            when_side(side, lambda side=side: row_copy(h, side).start())

    start_rows(0)
    for h in range(heads):
        pl.when(inner)(lambda h=h: z_copy(h).start())
        par_copy(h).start()
    for zc in range(2):
        w_own(zc).start()
        for step in (1, 3, 2):
            w_copy(step, zc).start()
    for h in range(heads):
        kvh[h, 1, 1:3] = kv_ref[h]

    def serve(h):
        for side in range(2):
            when_from(side, lambda side=side: row_copy(h, side).wait_recv())
        pl.when(inner)(lambda: z_copy(h).wait_recv())
        for side in range(2):
            when_from(side, lambda side=side: parcol_copy(h, side).start())
        for side in range(2):

            @pl.when(inner & (has_right if side == 0 else has_left))
            def _():
                zcol_copy(h, side).start()

        pl.when(h < heads - 1)(lambda: start_rows(h + 1))

    late = lax.broadcasted_iota(jnp.int32, (1, tokens), 1) >= tokens // 2
    n_rows = 2 + inner.astype(jnp.int32)

    def forward(c, h):
        ag_copy(c, h, c).wait_recv()
        ag_forward(c, h).start()

    def project(c):
        for h in range(heads):
            ag_copy(c, h, 1 - c).wait_recv()
            ag_forward(c, h).wait_recv()
        for b in range(tokens // SUB):
            at = slice(b * SUB, (b + 1) * SUB)
            lhs = jnp.concatenate(
                [ag[c, i, h, at] for i in range(NX) for h in range(heads)], axis=1
            )
            leave[c, at] = product(lhs, wg[1 - z], 1, 0).astype(BF16)
            sum_copy(c, b).start()
            part[c, at] = product(lhs, wg[z], 1, 0)

    def unit(u, carry):
        c, h = u // heads, lax.rem(u, heads)
        q = q_ref[h, c].astype(F32) * FACTOR
        q_high = q.astype(BF16)
        q2[:, :HEAD] = q_high
        q2[:, HEAD:] = (q - q_high.astype(F32)).astype(BF16)
        lanes = pl.ds(pl.multiple_of(h * HEAD, HEAD), HEAD)
        fold_chunk(
            q2, tk_ref[:, lanes], tv_ref[:, lanes], [None], m_ref, l_ref, acc_ref, s_ref, first=True
        )
        has_halo = jnp.where(c == 0, has_left.astype(jnp.int32), has_right.astype(jnp.int32))

        def visit(k, carry):
            @pl.when(k == 2)
            def _():
                pl.when(u == 0)(lambda: serve(0))
                pl.when(c == 0)(lambda: par_copy(h).wait_recv())

            @pl.when(k == 3)
            def _():
                @pl.when(u > 0)
                def _():
                    forward((u - 1) // heads, lax.rem(u - 1, heads))

                @pl.when(u == 1)
                def _():
                    for zc in range(2):
                        for step in (1, 3, 2):
                            w_copy(step, zc).wait_recv()
                            w_forward(step, zc).start()

            pl.when(k == 2 * n_rows + 1)(lambda: parcol_copy(h, c).wait_recv())
            pl.when(k == 2 * n_rows + 2)(lambda: zcol_copy(h, c).wait_recv())

            own = k < 2 * n_rows
            row_i = jnp.where(own, k // 2, k - 2 * n_rows)
            gap = jnp.where(own, lax.rem(k, 2), 1)
            row = jnp.where(row_i == 0, 1, jnp.where(row_i == 1, near, far))
            col = jnp.where(own, jnp.where(gap == 0, c + 1, 2 - c), 3 * c)
            away = (row_i > 0).astype(jnp.int32)
            pens = []
            for kt in range(2):
                pen = []
                for qt in range(2):
                    ok = (
                        (away <= radius[2 + qt, c])
                        & (gap <= radius[4 + qt, c])
                        & (abs(qt - kt) <= radius[qt, c])
                    )
                    pen.append(jnp.where(ok, 0.0, FAR))
                pens.append(jnp.where(late, pen[1], pen[0]))
            block = kvh.at[h, row, col]
            fold_chunk(q2, block[0], block[1], pens, m_ref, l_ref, acc_ref, s_ref)
            return carry

        lax.fori_loop(0, n_rows * (2 + has_halo), visit, 0)
        ag[c, x, h] = (acc_ref[...] / l_ref[...]).T.astype(BF16)
        for way in range(2):
            ag_copy(c, h, way).start()
        pl.when(u < heads - 1)(lambda: serve(u + 1))

        @pl.when(u == heads)
        def _():
            for zc in range(2):
                w_own(zc).wait()
                for step in (1, 3, 2):
                    w_forward(step, zc).wait_recv()

        @pl.when((u == heads) | (u == 2 * heads - 1))
        def _():
            pl.when(u > heads)(lambda: forward(1, heads - 1))
            project(c - (u == heads).astype(jnp.int32))

        return carry

    lax.fori_loop(0, 2 * heads, unit, 0)

    for c in range(2):
        for b in range(tokens // SUB):
            at = slice(b * SUB, (b + 1) * SUB)
            sum_copy(c, b).wait_recv()
            out_ref[c, at] = (part[c, at] + arrive[c, at].astype(F32)).astype(BF16)

    for c in range(2):
        for b in range(tokens // SUB):
            sum_copy(c, b).wait_send()
        for h in range(heads):
            ag_forward(c, h).wait_send()
            for way in range(2):
                ag_copy(c, h, way).wait_send()
    for zc in range(2):
        for step in range(1, NX):
            w_copy(step, zc).wait_send()
            w_forward(step, zc).wait_send()
    for h in range(heads):
        par_copy(h).wait_send()
        pl.when(inner)(lambda h=h: z_copy(h).wait_send())
        for side in range(2):
            when_side(side, lambda h=h, side=side: row_copy(h, side).wait_send())
            when_from(side, lambda h=h, side=side: parcol_copy(h, side).wait_send())

            @pl.when(inner & (has_right if side == 0 else has_left))
            def _():
                zcol_copy(h, side).wait_send()


def layer(radius, q, kv, text_keys, text_values, out_weight):
    heads, cols, tokens, _ = q.shape
    width = heads * HEAD
    dma = pltpu.SemaphoreType.DMA
    vmem = pl.BlockSpec(memory_space=pltpu.VMEM)
    blocks = tokens // SUB
    return pl.pallas_call(
        layer_kernel,
        in_specs=[
            pl.BlockSpec(memory_space=pltpu.SMEM),
            vmem, vmem, vmem, vmem,
            pl.BlockSpec(memory_space=pl.ANY),
        ],
        out_specs=vmem,
        out_shape=jax.ShapeDtypeStruct((cols, tokens, width), BF16),
        scratch_shapes=[
            pltpu.VMEM((heads, 3, 4, 2, tokens, HEAD), BF16),
            pltpu.VMEM((tokens, 2 * HEAD), BF16),
            pltpu.VMEM((1, tokens), F32),
            pltpu.VMEM((1, tokens), F32),
            pltpu.VMEM((HEAD, tokens), F32),
            pltpu.VMEM((blocks, tokens, SUB), F32),
            pltpu.VMEM((cols, NX, heads, tokens, HEAD), BF16),
            pltpu.VMEM((2, NX * width, width), BF16),
            pltpu.VMEM((cols, tokens, width), F32),
            pltpu.VMEM((cols, tokens, width), BF16),
            pltpu.VMEM((cols, tokens, width), BF16),
            dma((heads, 2)), dma((heads, 2)),
            dma((heads,)), dma((heads,)),
            dma((heads,)), dma((heads,)),
            dma((heads, 2)), dma((heads, 2)),
            dma((heads, 2)), dma((heads, 2)),
            dma((NX - 1, 2)), dma((NX - 1, 2)),
            dma((NX - 1, 2)), dma((NX - 1, 2)),
            dma((2,)),
            dma((cols, heads, 2)), dma((cols, heads, 2)),
            dma((cols, heads)), dma((cols, heads)),
            dma((cols, blocks)), dma((cols, blocks)),
        ],
        compiler_params=pltpu.CompilerParams(
            collective_id=0, has_side_effects=True, vmem_limit_bytes=60 * 1024 * 1024
        ),
        cost_estimate=pl.CostEstimate(
            flops=40_000_000_000, bytes_accessed=18_000_000, transcendentals=30_000_000
        ),
        name="layer",
    )(radius, q, kv, text_keys, text_values, out_weight)


def shards(queries, video_keys, video_values, text_keys, text_values, tile_radius, out_weight):
    n_frames, height, _, _ = queries.shape
    q = tiled(queries)
    kv = jnp.stack([tiled(video_keys), tiled(video_values)], axis=2)
    radius = tile_radius[:, :, 0, :].reshape(6, -1)
    return untiled(layer(radius, q, kv, text_keys, text_values, out_weight), n_frames, height)


def solution(mesh):
    placed = (
        P(None, "ha", "wa", "hd"),
        P(None, "ha", "wa", "hd"),
        P(None, "ha", "wa", "hd"),
        P(None, "hd"),
        P(None, "hd"),
        P(None, None, "ha", "wa"),
        P("hd", None),
    )
    return jax.shard_map(
        shards, mesh=mesh, in_specs=placed, out_specs=P(None, "ha", "wa", "hd"), check_vma=False
    )
```

time: 317 us -> 134 us (0.42)
  waiting for transfers between devices: 77.8 us -> 0 us
  blocking collectives: 63.9 us -> 0 us
  other arithmetic: 22.4 us -> 1.63 us
  local copies, waits for them, and re-layouts: 24 us -> 6.5 us
  Pallas kernels: 107 us -> 124 us
  starting transfers between devices: 12.8 us -> 0 us
  matrix products: 8.95 us -> 0 us
    ppermute x4 -> x0, waiting for transfers between devices: 77.8 us -> none  [the longest x2 70.6 us: shifts(): lax.ppermute(block[0], axis, forward)]
    all_to_all x1 -> x0, blocking collectives: 63.9 us -> none  [summed_on_arrival(): lax.all_to_all(blocks, axis, split_axis=0, concat_axis=0, tiled=True)]
    pallas_call x1, Pallas kernels: 107 us -> 124 us  [layer(): pl.pallas_call(layer_kernel, in_specs=[pl.BlockSpec(memory_space=pltpu.SM...]
    another operation x2 -> x1, other arithmetic: 16.8 us -> 1.63 us  [shards(): kv = jnp.stack([tiled(video_keys), tiled(video_values)], axis=2)]
    ppermute x4 -> x0, starting transfers between devices: 12.8 us -> none  [the longest x2 8.27 us: shifts(): lax.ppermute(block[0], axis, forward)]
    unnamed x9 -> x6, local copies, waits for them, and re-layouts: 9.66 us -> 0.01 us
    dot_general x1 -> x0, matrix products: 8.95 us -> none  [shards(): jnp.dot(mixture.reshape(-1, channels), out_weight, preferred_element_type...]
    another operation x1 -> x0, local copies, waits for them, and re-layouts: 8.87 us -> none  [summed_on_arrival(): value.reshape(*shape[:dim], size, shape[dim] // size, *shape[dim + 1:])]
  transfers between devices with their start and end apart: 4 -> 0, of which waited for: 4 -> 0; matrix products, arithmetic and copies ran while one was open for 1% -> 0% of each run, Pallas kernels for 0% -> 0%
where the time goes in v2:
time: 134 us; the launch traced here: 132 us
  Pallas kernels  124 us (93%)
  local copies, waits for them, and re-layouts  6.5 us (5%)
  other arithmetic  1.63 us (1%)
    pallas_call x1, Pallas kernels, layer(): pl.pallas_call(layer_kernel, in_specs=[pl.BlockSpec(memory_space=pltpu.SM...  124 us
    reshape x3, local copies, waits for them, and re-layouts, tiled(): cut = block.reshape(frames, height, cols, TILE_W, heads, HEAD)  3.38 us

profile of v2, /device:TPU:17, one launch (start us, length us, event | category | flops | bytes accessed | tf_op | source)
XLA Modules:
  0.0 131.8 jit_solution(3857190460985701444)
XLA Ops:
  0.0 0.0 copy-start
  0.0 1.7 %copy.16 = bf16[12,8,2,8,3,128]{5,3,1,0,2,4:T(8,128)(2,1)S(1)} copy(bf16[12,8,2,8,3,128]{5,3,4,2,1,0:T(8,128)(2,1)} %bitcast.22) | data formatting | bytes 2359296 | tf_op jit(solution)/shard_map/reshape | solution.py:25
  1.7 0.0 copy-done
  1.7 0.3 copy.17
  2.1 0.0 copy-start.1
  2.1 1.6 %pad_maximum_fusion.kv_ref = bf16[3,2,2,768,128]{4,3,2,1,0:T(8,128)(2,1)} fusion(bf16[3,2,1,768,128]{4,3,2,1,0:T(8,128)(2,1)S(1)} %bitcast.21, bf16[3,2,1,768,128]{4,3,2,1,0:T(8,128)(2,1)S(1)} %bitcast.20), kind=kLoop, calls=%fused_computation | loop fusion | flops 1179648 | bytes 4718592 | tf_op jit(solution)/shard_map/stack | solution.py:407
  3.7 0.0 copy-done.1
  3.7 0.0 copy-start.2
  3.7 1.4 %copy.15 = bf16[12,8,2,8,3,128]{5,3,1,0,2,4:T(8,128)(2,1)} copy(bf16[12,8,2,8,3,128]{5,3,4,2,1,0:T(8,128)(2,1)S(1)} %bitcast.24) | data formatting | bytes 2359296 | tf_op jit(solution)/shard_map/reshape | solution.py:25
  5.1 0.0 copy-done.2
  5.1 0.1 copy.20
  5.2 0.6 reshape.24.radius
  5.8 123.6 %layer.1 = bf16[2,768,384]{2,1,0:T(8,128)(2,1)} custom-call(s32[6,2]{1,0:T(8,128)} %reshape.24.radius, bf16[3,2,768,128]{3,2,1,0:T(8,128)(2,1)} %bitcast.25, bf16[3,2,2,768,128]{4,3,2,1,0:T(8,128)(2,1)} %pad_maximum_fusion.kv_ref, bf16[256,384]{1,0:T(8,128)(2,1)} %tk_ref.1, bf16[256,384]{1,0:T(8,128)(2,1)} %tv_ref.1, bf16[384,3072]{1,0:T(8,128)(2,1)} %w_ref.1), custom_call_target="tpu_custom_call" | custom-call | flops 40000000000 | bytes 18000000 | tf_op jit(solution)/shard_map/layer/pallas_call | solution.py:361
  129.4 2.4 %copy.23 = bf16[12,8,2,8,384]{4,3,2,1,0:T(8,128)(2,1)} copy(bf16[12,8,2,8,384]{4,3,1,0,2:T(8,128)(2,1)} %bitcast.26) | data formatting | bytes 2359296 | tf_op jit(solution)/shard_map/transpose | solution.py:32
Async XLA Ops:
  0.0 1.7 %copy-start = (bf16[12,8,16,384]{3,2,1,0:T(8,128)(2,1)S(1)}, bf16[12,8,16,384]{3,2,1,0:T(8,128)(2,1)}, u32[]{:S(2)}) copy-start(bf16[12,8,16,384]{3,2,1,0:T(8,128)(2,1)} %param.9) | copy-start | bytes 3538948
  2.1 1.6 %copy-start.1 = (bf16[12,8,16,384]{3,2,1,0:T(8,128)(2,1)S(1)}, bf16[12,8,16,384]{3,2,1,0:T(8,128)(2,1)}, u32[]{:S(2)}) copy-start(bf16[12,8,16,384]{3,2,1,0:T(8,128)(2,1)} %param.7) | copy-start | bytes 3538948
  3.7 1.4 %copy-start.2 = (s32[3,2,1,2]{0,3,2,1:T(2,128)S(1)}, s32[3,2,1,2]{0,3,2,1:T(2,128)}, u32[]{:S(2)}) copy-start(s32[3,2,1,2]{0,3,2,1:T(2,128)} %param.12) | copy-start | bytes 148

commit v3 on v2

--- a/solution.py
+++ b/solution.py
@@ -11,6 +11,8 @@
 TILE_W = 8
 FACTOR = 1.4426950408889634 * HEAD ** (-0.5)
 FAR = 1e30
+LOG3 = 1.5849625007211562
+TEXT_SLOT = 12
 SUB = 256
 NX = 4
 BF16 = jnp.bfloat16
@@ -36,47 +38,53 @@
     return lax.dot_general(a, b, (((over_a,), (over_b,)), ((), ())), preferred_element_type=F32)
 
 
-def fold_chunk(q2, k, v, pens, m_ref, l_ref, acc_ref, s_ref, first=False):
-    count = len(pens)
-    keys = k.shape[0] // count
-    k2 = jnp.concatenate([k, k], axis=1)
-    for part, start in enumerate(range(0, q2.shape[0], SUB)):
-        at = slice(start, start + SUB)
-        s = product(k2, q2[at], 1, 1)
-        held = s_ref.at[part]
-        held[: k.shape[0]] = s
-        tops = [
-            jnp.max(s[i * keys : (i + 1) * keys], axis=0, keepdims=True) for i in range(count)
-        ]
-        rows = [None if pen is None else pen[:, at] for pen in pens]
-        tops = [top if row is None else top - row for top, row in zip(tops, rows)]
-        m_new = functools.reduce(jnp.maximum, tops)
-        if not first:
-            m_old = m_ref[:, at]
-            m_new = jnp.maximum(m_new, m_old)
-        weights = [
-            jnp.exp2(held[i * keys : (i + 1) * keys] - (m_new if row is None else m_new + row))
-            for i, row in enumerate(rows)
-        ]
-        total = functools.reduce(
-            jnp.add, [jnp.sum(weight, axis=0, keepdims=True) for weight in weights]
-        )
-        low = [weight.astype(BF16) for weight in weights]
-        low = low[0] if count == 1 else jnp.concatenate(low, axis=0)
-        add = product(v, low, 0, 0)
-        if first:
-            l_ref[:, at] = total
-            acc_ref[:, at] = add
-        else:
-            shrink = jnp.exp2(m_old - m_new)
-            l_ref[:, at] = l_ref[:, at] * shrink + total
-            acc_ref[:, at] = acc_ref[:, at] * shrink + add
-        m_ref[:, at] = m_new
+def score_part(q2, k, part, s_ref, top_ref):
+    at = slice(part * SUB, (part + 1) * SUB)
+    s = product(jnp.concatenate([k, k], axis=1), q2[at], 1, 1)
+    s_ref[...] = s
+    keys = k.shape[0] // 2
+    for t in range(2):
+        top_ref[t : t + 1, at] = jnp.max(s[t * keys : (t + 1) * keys], axis=0, keepdims=True)
+
+
+def blend_part(v, pens, part, s_ref, top_ref, m_ref, l_ref, acc_ref):
+    at = slice(part * SUB, (part + 1) * SUB)
+    keys = v.shape[0] // 2
+    rows = [pen[:, at] for pen in pens]
+    m_old = m_ref[:, at]
+    m_new = m_old
+    for t in range(2):
+        m_new = jnp.maximum(m_new, top_ref[t : t + 1, at] - rows[t])
+    weights = [
+        jnp.exp2(s_ref[t * keys : (t + 1) * keys] - (m_new + rows[t])) for t in range(2)
+    ]
+    total = sum(jnp.sum(weight, axis=0, keepdims=True) for weight in weights)
+    low = jnp.concatenate([weight.astype(BF16) for weight in weights], axis=0)
+    shrink = jnp.exp2(m_old - m_new)
+    l_ref[:, at] = l_ref[:, at] * shrink + total
+    acc_ref[:, at] = acc_ref[:, at] * shrink + product(v, low, 0, 0)
+    m_ref[:, at] = m_new
+
+
+def pair_at(p):
+    unit = p // 2
+    pair = lax.rem(p, 2)
+    for start, count, first_unit, first_pair in (
+        (8, 3, 0, 2), (14, 2, 4, 0), (18, 3, 2, 2), (24, 2, 4, 2), (28, 1, 4, 4),
+    ):
+        here = p >= start
+        unit = jnp.where(here, first_unit + (p - start) // count, unit)
+        pair = jnp.where(here, first_pair + lax.rem(p - start, count), pair)
+    return unit, pair
+
+
+STEPS = 30
 
 
 def layer_kernel(
     radius, q_ref, kv_ref, tk_ref, tv_ref, w_ref, out_ref,
-    kvh, q2, m_ref, l_ref, acc_ref, s_ref, ag, wg, part, leave, arrive,
+    kvh, q2, m_ref, l_ref, acc_ref, top0, top1, s00, s01, s02, s10, s11, s12,
+    ag, wg, part, part_far, leave, arrive,
     row_s, row_r, par_s, par_r, z_s, z_r, parcol_s, parcol_r, zcol_s, zcol_r,
     w_s, w_r, wf_s, wf_r, wl, ag_s, ag_r, agf_s, agf_r, sum_s, sum_r,
 ):
@@ -107,29 +115,29 @@
 
     def row_copy(h, side):
         return remote(
-            kv_ref.at[h, 1 - side], kvh.at[h, 1, 3 * side], row_s.at[h, side], row_r.at[h, side],
+            kv_ref.at[h, 1 - side], kvh.at[h, 4 + 3 * side], row_s.at[h, side], row_r.at[h, side],
             {"wa": wa + 1 - 2 * side},
         )
 
     def par_copy(h):
         return remote(
-            kv_ref.at[h], kvh.at[h, far, pl.ds(1, 2)], par_s.at[h], par_r.at[h], {"ha": partner}
+            kv_ref.at[h], kvh.at[h, pl.ds(4 * far + 1, 2)], par_s.at[h], par_r.at[h], {"ha": partner}
         )
 
     def z_copy(h):
         return remote(
-            kv_ref.at[h], kvh.at[h, near, pl.ds(1, 2)], z_s.at[h], z_r.at[h], {"ha": peer}
+            kv_ref.at[h], kvh.at[h, pl.ds(4 * near + 1, 2)], z_s.at[h], z_r.at[h], {"ha": peer}
         )
 
     def parcol_copy(h, side):
         return remote(
-            kvh.at[h, 1, 3 * side], kvh.at[h, far, 3 * side],
+            kvh.at[h, 4 + 3 * side], kvh.at[h, 4 * far + 3 * side],
             parcol_s.at[h, side], parcol_r.at[h, side], {"ha": partner},
         )
 
     def zcol_copy(h, side):
         return remote(
-            kvh.at[h, far, 2 - side], kvh.at[h, far, 3 * side],
+            kvh.at[h, 4 * far + 2 - side], kvh.at[h, 4 * far + 3 * side],
             zcol_s.at[h, side], zcol_r.at[h, side], {"wa": wa + 1 - 2 * side},
         )
 
@@ -210,7 +218,20 @@
         for step in (1, 3, 2):
             w_copy(step, zc).start()
     for h in range(heads):
-        kvh[h, 1, 1:3] = kv_ref[h]
+        kvh[h, 5:7] = kv_ref[h]
+        lanes = slice(h * HEAD, (h + 1) * HEAD)
+        for copy in range(3):
+            rows = slice(copy * SUB, (copy + 1) * SUB)
+            kvh[h, TEXT_SLOT, 0, rows] = tk_ref[:, lanes]
+            kvh[h, TEXT_SLOT, 1, rows] = tv_ref[:, lanes]
+    for u in range(2 * heads):
+        q = q_ref[u // 2, u % 2].astype(F32) * FACTOR
+        q_high = q.astype(BF16)
+        q2[u, :, :HEAD] = q_high
+        q2[u, :, HEAD:] = (q - q_high.astype(F32)).astype(BF16)
+    m_ref[...] = jnp.full_like(m_ref, -FAR)
+    l_ref[...] = jnp.zeros_like(l_ref)
+    acc_ref[...] = jnp.zeros_like(acc_ref)
 
     def serve(h):
         for side in range(2):
@@ -227,101 +248,145 @@
         pl.when(h < heads - 1)(lambda: start_rows(h + 1))
 
     late = lax.broadcasted_iota(jnp.int32, (1, tokens), 1) >= tokens // 2
-    n_rows = 2 + inner.astype(jnp.int32)
-
-    def forward(c, h):
+    sets = ((s00, s01, s02), (s10, s11, s12))
+    peaks = (top0, top1)
+    parts = tokens // SUB
+
+    def halo_at(c):
+        return jnp.where(c == 0, has_left.astype(jnp.int32), has_right.astype(jnp.int32))
+
+    def chunk_at(c, chunk):
+        v = chunk - 1
+        side_col = v >= 6
+        row_i = jnp.where(side_col, v - 6, v // 2)
+        gap = jnp.where(side_col, 1, lax.rem(v, 2))
+        there = ((row_i < 2) | inner) & ((v < 6) | (halo_at(c) > 0))
+        row = jnp.where(row_i == 0, 1, jnp.where(row_i == 1, near, far))
+        col = jnp.where(side_col, 3 * c, jnp.where(gap == 0, c + 1, 2 - c))
+        slot = jnp.where(there, 4 * row + col, 5 + c)
+        slot = jnp.where(chunk == 0, TEXT_SLOT, slot)
+        return slot, there, (row_i > 0).astype(jnp.int32), gap
+
+    def score_step(u, pair, which, part_i):
+        slot, _, _, _ = chunk_at(lax.rem(u, 2), 2 * pair + which)
+        score_part(q2.at[u], kvh[u // 2, slot, 0], part_i, sets[which][part_i], peaks[which])
+
+    def pens_of(u, pair, which):
+        c = lax.rem(u, 2)
+        chunk = 2 * pair + which
+        _, there, away, gap = chunk_at(c, chunk)
+        pens = []
+        for kt in range(2):
+            pen = []
+            for qt in range(2):
+                ok = (
+                    there
+                    & (away <= radius[2 + qt, c])
+                    & (gap <= radius[4 + qt, c])
+                    & (abs(qt - kt) <= radius[qt, c])
+                )
+                pen.append(jnp.where(chunk == 0, LOG3, jnp.where(ok, 0.0, FAR)))
+            pens.append(jnp.where(late, pen[1], pen[0]))
+        return pens
+
+    def forward(u):
+        h, c = u // 2, lax.rem(u, 2)
         ag_copy(c, h, c).wait_recv()
         ag_forward(c, h).start()
 
-    def project(c):
-        for h in range(heads):
-            ag_copy(c, h, 1 - c).wait_recv()
-            ag_forward(c, h).wait_recv()
-        for b in range(tokens // SUB):
+    def gathered(c, h):
+        ag_copy(c, h, 1 - c).wait_recv()
+        ag_forward(c, h).wait_recv()
+
+    def rows_of(zc, h):
+        return [wg[zc, i * width + h * HEAD : i * width + (h + 1) * HEAD] for i in range(NX)]
+
+    def last_rows(zc):
+        return jnp.concatenate(rows_of(zc, heads - 1), axis=0)
+
+    def project_first(c):
+        for h in range(heads - 1):
+            gathered(c, h)
+        for b in range(parts):
             at = slice(b * SUB, (b + 1) * SUB)
             lhs = jnp.concatenate(
-                [ag[c, i, h, at] for i in range(NX) for h in range(heads)], axis=1
+                [ag[c, i, h, at] for h in range(heads - 1) for i in range(NX)], axis=1
             )
-            leave[c, at] = product(lhs, wg[1 - z], 1, 0).astype(BF16)
+            for zc, out in ((1 - z, part_far), (z, part)):
+                rhs = [block for h in range(heads - 1) for block in rows_of(zc, h)]
+                out[c, at] = product(lhs, jnp.concatenate(rhs, axis=0), 1, 0)
+
+    def project_last(c):
+        h = heads - 1
+        gathered(c, h)
+        for b in range(parts):
+            at = slice(b * SUB, (b + 1) * SUB)
+            lhs = jnp.concatenate([ag[c, i, h, at] for i in range(NX)], axis=1)
+            leave[c, at] = (part_far[c, at] + product(lhs, last_rows(1 - z), 1, 0)).astype(BF16)
             sum_copy(c, b).start()
-            part[c, at] = product(lhs, wg[z], 1, 0)
-
-    def unit(u, carry):
-        c, h = u // heads, lax.rem(u, heads)
-        q = q_ref[h, c].astype(F32) * FACTOR
-        q_high = q.astype(BF16)
-        q2[:, :HEAD] = q_high
-        q2[:, HEAD:] = (q - q_high.astype(F32)).astype(BF16)
-        lanes = pl.ds(pl.multiple_of(h * HEAD, HEAD), HEAD)
-        fold_chunk(
-            q2, tk_ref[:, lanes], tv_ref[:, lanes], [None], m_ref, l_ref, acc_ref, s_ref, first=True
-        )
-        has_halo = jnp.where(c == 0, has_left.astype(jnp.int32), has_right.astype(jnp.int32))
-
-        def visit(k, carry):
-            @pl.when(k == 2)
-            def _():
-                pl.when(u == 0)(lambda: serve(0))
-                pl.when(c == 0)(lambda: par_copy(h).wait_recv())
-
-            @pl.when(k == 3)
-            def _():
-                @pl.when(u > 0)
-                def _():
-                    forward((u - 1) // heads, lax.rem(u - 1, heads))
-
-                @pl.when(u == 1)
-                def _():
-                    for zc in range(2):
-                        for step in (1, 3, 2):
-                            w_copy(step, zc).wait_recv()
-                            w_forward(step, zc).start()
-
-            pl.when(k == 2 * n_rows + 1)(lambda: parcol_copy(h, c).wait_recv())
-            pl.when(k == 2 * n_rows + 2)(lambda: zcol_copy(h, c).wait_recv())
-
-            own = k < 2 * n_rows
-            row_i = jnp.where(own, k // 2, k - 2 * n_rows)
-            gap = jnp.where(own, lax.rem(k, 2), 1)
-            row = jnp.where(row_i == 0, 1, jnp.where(row_i == 1, near, far))
-            col = jnp.where(own, jnp.where(gap == 0, c + 1, 2 - c), 3 * c)
-            away = (row_i > 0).astype(jnp.int32)
-            pens = []
-            for kt in range(2):
-                pen = []
-                for qt in range(2):
-                    ok = (
-                        (away <= radius[2 + qt, c])
-                        & (gap <= radius[4 + qt, c])
-                        & (abs(qt - kt) <= radius[qt, c])
-                    )
-                    pen.append(jnp.where(ok, 0.0, FAR))
-                pens.append(jnp.where(late, pen[1], pen[0]))
-            block = kvh.at[h, row, col]
-            fold_chunk(q2, block[0], block[1], pens, m_ref, l_ref, acc_ref, s_ref)
-            return carry
-
-        lax.fori_loop(0, n_rows * (2 + has_halo), visit, 0)
-        ag[c, x, h] = (acc_ref[...] / l_ref[...]).T.astype(BF16)
-        for way in range(2):
-            ag_copy(c, h, way).start()
-        pl.when(u < heads - 1)(lambda: serve(u + 1))
-
-        @pl.when(u == heads)
+        for b in range(parts):
+            at = slice(b * SUB, (b + 1) * SUB)
+            lhs = jnp.concatenate([ag[c, i, h, at] for i in range(NX)], axis=1)
+            part[c, at] = part[c, at] + product(lhs, last_rows(z), 1, 0)
+
+    for which in range(2):
+        for part_i in range(parts):
+            score_step(0, 0, which, part_i)
+
+    def step(p, carry):
+        u, pair = pair_at(p)
+        u_next, pair_next = pair_at(jnp.minimum(p + 1, STEPS - 1))
+        h_next, c_next = u_next // 2, lax.rem(u_next, 2)
+        pl.when((pair_next == 1) & (c_next == 0))(lambda: par_copy(h_next).wait_recv())
+        for at_step, h in ((6, 0), (16, 1), (23, 2)):
+            pl.when(p == at_step)(lambda h=h: serve(h))
+
+        @pl.when((pair_next == 4) & (p < STEPS - 1) & (halo_at(c_next) > 0))
+        def _():
+            parcol_copy(h_next, c_next).wait_recv()
+            pl.when(inner)(lambda: zcol_copy(h_next, c_next).wait_recv())
+
+        @pl.when(p == 17)
         def _():
             for zc in range(2):
-                w_own(zc).wait()
-                for step in (1, 3, 2):
-                    w_forward(step, zc).wait_recv()
-
-        @pl.when((u == heads) | (u == 2 * heads - 1))
+                for hop in (1, 3, 2):
+                    w_copy(hop, zc).wait_recv()
+                    w_forward(hop, zc).start()
+
+        for at_step, done in ((16, 0), (19, 1), (26, 2), (29, 3)):
+            pl.when(p == at_step)(lambda done=done: forward(jnp.int32(done)))
+
+        pens = [pens_of(u, pair, which) for which in range(2)]
+        c, h = lax.rem(u, 2), u // 2
+        for which in range(2):
+            slot, _, _, _ = chunk_at(c, 2 * pair + which)
+            for part_i in range(parts):
+                blend_part(
+                    kvh[h, slot, 1], pens[which], part_i, sets[which][part_i], peaks[which],
+                    m_ref.at[u], l_ref.at[u], acc_ref.at[u],
+                )
+                score_step(u_next, pair_next, which, part_i)
+
+        @pl.when(pair == 4)
         def _():
-            pl.when(u > heads)(lambda: forward(1, heads - 1))
-            project(c - (u == heads).astype(jnp.int32))
+            ag[c, x, h] = (acc_ref[u] / l_ref[u]).T.astype(BF16)
+            for way in range(2):
+                ag_copy(c, h, way).start()
 
         return carry
 
-    lax.fori_loop(0, 2 * heads, unit, 0)
+    lax.fori_loop(0, STEPS, step, 0)
+
+    for zc in range(2):
+        w_own(zc).wait()
+        for hop in (1, 3, 2):
+            w_forward(hop, zc).wait_recv()
+    project_first(0)
+    forward(jnp.int32(4))
+    project_first(1)
+    forward(jnp.int32(5))
+    project_last(0)
+    project_last(1)
 
     for c in range(2):
         for b in range(tokens // SUB):
@@ -368,14 +433,17 @@
         out_specs=vmem,
         out_shape=jax.ShapeDtypeStruct((cols, tokens, width), BF16),
         scratch_shapes=[
-            pltpu.VMEM((heads, 3, 4, 2, tokens, HEAD), BF16),
-            pltpu.VMEM((tokens, 2 * HEAD), BF16),
-            pltpu.VMEM((1, tokens), F32),
-            pltpu.VMEM((1, tokens), F32),
-            pltpu.VMEM((HEAD, tokens), F32),
-            pltpu.VMEM((blocks, tokens, SUB), F32),
+            pltpu.VMEM((heads, TEXT_SLOT + 1, 2, tokens, HEAD), BF16),
+            pltpu.VMEM((2 * heads, tokens, 2 * HEAD), BF16),
+            pltpu.VMEM((2 * heads, 1, tokens), F32),
+            pltpu.VMEM((2 * heads, 1, tokens), F32),
+            pltpu.VMEM((2 * heads, HEAD, tokens), F32),
+            pltpu.VMEM((2, tokens), F32),
+            pltpu.VMEM((2, tokens), F32),
+            *[pltpu.VMEM((tokens, SUB), F32)] * (2 * blocks),
             pltpu.VMEM((cols, NX, heads, tokens, HEAD), BF16),
             pltpu.VMEM((2, NX * width, width), BF16),
+            pltpu.VMEM((cols, tokens, width), F32),
             pltpu.VMEM((cols, tokens, width), F32),
             pltpu.VMEM((cols, tokens, width), BF16),
             pltpu.VMEM((cols, tokens, width), BF16),

time: 134 us -> 111 us (0.83); the launches traced: 132 us -> 111 us
  Pallas kernels: 124 us -> 103 us
    pallas_call x1, Pallas kernels: 124 us -> 103 us  [layer(): pl.pallas_call(layer_kernel, in_specs=[pl.BlockSpec(memory_space=pltpu.SM...]
where the time goes in v3:
time: 111 us
  Pallas kernels  103 us (93%)
  local copies, waits for them, and re-layouts  6.5 us (6%)
  other arithmetic  1.63 us (1%)
    pallas_call x1, Pallas kernels, layer(): pl.pallas_call(layer_kernel, in_specs=[pl.BlockSpec(memory_space=pltpu.SM...  103 us
    reshape x3, local copies, waits for them, and re-layouts, tiled(): cut = block.reshape(frames, height, cols, TILE_W, heads, HEAD)  3.38 us
    transpose x1, local copies, waits for them, and re-layouts, untiled(): cut.transpose(1, 2, 0, 3, 4)  2.41 us

profile of v3, /device:TPU:17, one launch (start us, length us, event | category | flops | bytes accessed | tf_op | source)
XLA Modules:
  0.0 111.0 jit_solution(11355959001950916466)
XLA Ops:
  0.0 0.0 copy-start
  0.0 1.7 %copy.16 = bf16[12,8,2,8,3,128]{5,3,1,0,2,4:T(8,128)(2,1)S(1)} copy(bf16[12,8,2,8,3,128]{5,3,4,2,1,0:T(8,128)(2,1)} %bitcast.22) | data formatting | bytes 2359296 | tf_op jit(solution)/shard_map/reshape | solution.py:27
  1.7 0.0 copy-done
  1.7 0.3 copy.17
  2.1 0.0 copy-start.1
  2.1 1.6 %pad_maximum_fusion.kv_ref = bf16[3,2,2,768,128]{4,3,2,1,0:T(8,128)(2,1)} fusion(bf16[3,2,1,768,128]{4,3,2,1,0:T(8,128)(2,1)S(1)} %bitcast.21, bf16[3,2,1,768,128]{4,3,2,1,0:T(8,128)(2,1)S(1)} %bitcast.20), kind=kLoop, calls=%fused_computation | loop fusion | flops 1179648 | bytes 4718592 | tf_op jit(solution)/shard_map/stack | solution.py:475
  3.7 0.0 copy-done.1
  3.7 0.0 copy-start.2
  3.7 1.4 %copy.15 = bf16[12,8,2,8,3,128]{5,3,1,0,2,4:T(8,128)(2,1)} copy(bf16[12,8,2,8,3,128]{5,3,4,2,1,0:T(8,128)(2,1)S(1)} %bitcast.24) | data formatting | bytes 2359296 | tf_op jit(solution)/shard_map/reshape | solution.py:27
  5.1 0.0 copy-done.2
  5.1 0.1 copy.20
  5.2 0.6 reshape.24.radius
  5.8 102.8 %layer.1 = bf16[2,768,384]{2,1,0:T(8,128)(2,1)} custom-call(s32[6,2]{1,0:T(8,128)} %reshape.24.radius, bf16[3,2,768,128]{3,2,1,0:T(8,128)(2,1)} %bitcast.25, bf16[3,2,2,768,128]{4,3,2,1,0:T(8,128)(2,1)} %pad_maximum_fusion.kv_ref, bf16[256,384]{1,0:T(8,128)(2,1)} %tk_ref.1, bf16[256,384]{1,0:T(8,128)(2,1)} %tv_ref.1, bf16[384,3072]{1,0:T(8,128)(2,1)} %w_ref.1), custom_call_target="tpu_custom_call" | custom-call | flops 40000000000 | bytes 18000000 | tf_op jit(solution)/shard_map/layer/pallas_call | solution.py:426
  108.6 2.4 %copy.23 = bf16[12,8,2,8,384]{4,3,2,1,0:T(8,128)(2,1)} copy(bf16[12,8,2,8,384]{4,3,1,0,2:T(8,128)(2,1)} %bitcast.26) | data formatting | bytes 2359296 | tf_op jit(solution)/shard_map/transpose | solution.py:34
Async XLA Ops:
  0.0 1.7 %copy-start = (bf16[12,8,16,384]{3,2,1,0:T(8,128)(2,1)S(1)}, bf16[12,8,16,384]{3,2,1,0:T(8,128)(2,1)}, u32[]{:S(2)}) copy-start(bf16[12,8,16,384]{3,2,1,0:T(8,128)(2,1)} %param.9) | copy-start | bytes 3538948
  2.1 1.6 %copy-start.1 = (bf16[12,8,16,384]{3,2,1,0:T(8,128)(2,1)S(1)}, bf16[12,8,16,384]{3,2,1,0:T(8,128)(2,1)}, u32[]{:S(2)}) copy-start(bf16[12,8,16,384]{3,2,1,0:T(8,128)(2,1)} %param.7) | copy-start | bytes 3538948
  3.7 1.4 %copy-start.2 = (s32[3,2,1,2]{0,3,2,1:T(2,128)S(1)}, s32[3,2,1,2]{0,3,2,1:T(2,128)}, u32[]{:S(2)}) copy-start(s32[3,2,1,2]{0,3,2,1:T(2,128)} %param.12) | copy-start | bytes 148

commit v4 on v3

--- a/solution.py
+++ b/solution.py
@@ -66,15 +66,20 @@
     m_ref[:, at] = m_new
 
 
+ORDER = (
+    (0, 0, 2), (1, 0, 2), (0, 2, 2), (1, 2, 2), (2, 0, 2), (0, 4, 1), (1, 4, 1), (2, 2, 1),
+    (3, 0, 2), (2, 3, 1), (3, 2, 2), (2, 4, 1), (3, 4, 1), (4, 0, 5), (5, 0, 5),
+)
+
+
 def pair_at(p):
-    unit = p // 2
-    pair = lax.rem(p, 2)
-    for start, count, first_unit, first_pair in (
-        (8, 3, 0, 2), (14, 2, 4, 0), (18, 3, 2, 2), (24, 2, 4, 2), (28, 1, 4, 4),
-    ):
-        here = p >= start
-        unit = jnp.where(here, first_unit + (p - start) // count, unit)
-        pair = jnp.where(here, first_pair + lax.rem(p - start, count), pair)
+    unit, pair, start = jnp.int32(0), p, 0
+    for run_unit, first, count in ORDER:
+        if start > 0:
+            here = p >= start
+            unit = jnp.where(here, run_unit, unit)
+            pair = jnp.where(here, p + (first - start), pair)
+        start += count
     return unit, pair
 
 
@@ -86,7 +91,7 @@
     kvh, q2, m_ref, l_ref, acc_ref, top0, top1, s00, s01, s02, s10, s11, s12,
     ag, wg, part, part_far, leave, arrive,
     row_s, row_r, par_s, par_r, z_s, z_r, parcol_s, parcol_r, zcol_s, zcol_r,
-    w_s, w_r, wf_s, wf_r, wl, ag_s, ag_r, agf_s, agf_r, sum_s, sum_r,
+    w_s, w_r, wf_s, wf_r, wl, ag_s, ag_r, agf_s, agf_r, end_s, end_r, sum_s, sum_r,
 ):
     heads = q_ref.shape[0]
     tokens = q_ref.shape[2]
@@ -172,6 +177,12 @@
         block = ag.at[c, lax.rem(x + NX - 1 + 2 * c, NX), h]
         return remote(
             block, block, agf_s.at[c, h], agf_r.at[c, h], {"hd": x_at(1 + 2 * c)}
+        )
+
+    def end_copy(c, b, hop):
+        block = ag.at[c, x, heads - 1, pl.ds(b * SUB, SUB)]
+        return remote(
+            block, block, end_s.at[c, b, hop - 1], end_r.at[c, b, hop - 1], {"hd": x_at(hop)}
         )
 
     def sum_copy(c, b):
@@ -233,19 +244,20 @@
     l_ref[...] = jnp.zeros_like(l_ref)
     acc_ref[...] = jnp.zeros_like(acc_ref)
 
-    def serve(h):
+    def serve_z(h):
+        z_copy(h).wait_recv()
         for side in range(2):
-            when_from(side, lambda side=side: row_copy(h, side).wait_recv())
-        pl.when(inner)(lambda: z_copy(h).wait_recv())
+            when_side(side, lambda side=side: zcol_copy(h, side).start())
+        if h < heads - 1:
+            start_rows(h + 1)
+
+    def serve_rows(h):
         for side in range(2):
-            when_from(side, lambda side=side: parcol_copy(h, side).start())
-        for side in range(2):
-
-            @pl.when(inner & (has_right if side == 0 else has_left))
-            def _():
-                zcol_copy(h, side).start()
-
-        pl.when(h < heads - 1)(lambda: start_rows(h + 1))
+
+            @pl.when(has_left if side == 0 else has_right)
+            def _(side=side):
+                row_copy(h, side).wait_recv()
+                parcol_copy(h, side).start()
 
     late = lax.broadcasted_iota(jnp.int32, (1, tokens), 1) >= tokens // 2
     sets = ((s00, s01, s02), (s10, s11, s12))
@@ -294,10 +306,6 @@
         ag_copy(c, h, c).wait_recv()
         ag_forward(c, h).start()
 
-    def gathered(c, h):
-        ag_copy(c, h, 1 - c).wait_recv()
-        ag_forward(c, h).wait_recv()
-
     def rows_of(zc, h):
         return [wg[zc, i * width + h * HEAD : i * width + (h + 1) * HEAD] for i in range(NX)]
 
@@ -306,7 +314,8 @@
 
     def project_first(c):
         for h in range(heads - 1):
-            gathered(c, h)
+            ag_copy(c, h, 1 - c).wait_recv()
+            ag_forward(c, h).wait_recv()
         for b in range(parts):
             at = slice(b * SUB, (b + 1) * SUB)
             lhs = jnp.concatenate(
@@ -316,45 +325,55 @@
                 rhs = [block for h in range(heads - 1) for block in rows_of(zc, h)]
                 out[c, at] = product(lhs, jnp.concatenate(rhs, axis=0), 1, 0)
 
-    def project_last(c):
-        h = heads - 1
-        gathered(c, h)
-        for b in range(parts):
-            at = slice(b * SUB, (b + 1) * SUB)
-            lhs = jnp.concatenate([ag[c, i, h, at] for i in range(NX)], axis=1)
-            leave[c, at] = (part_far[c, at] + product(lhs, last_rows(1 - z), 1, 0)).astype(BF16)
-            sum_copy(c, b).start()
-        for b in range(parts):
-            at = slice(b * SUB, (b + 1) * SUB)
-            lhs = jnp.concatenate([ag[c, i, h, at] for i in range(NX)], axis=1)
-            part[c, at] = part[c, at] + product(lhs, last_rows(z), 1, 0)
+    def project_last(c, b):
+        for hop in (1, 3, 2):
+            end_copy(c, b, hop).wait_recv()
+        at = slice(b * SUB, (b + 1) * SUB)
+        lhs = jnp.concatenate([ag[c, i, heads - 1, at] for i in range(NX)], axis=1)
+        leave[c, at] = (part_far[c, at] + product(lhs, last_rows(1 - z), 1, 0)).astype(BF16)
+        sum_copy(c, b).start()
+        part[c, at] = part[c, at] + product(lhs, last_rows(z), 1, 0)
 
     for which in range(2):
         for part_i in range(parts):
             score_step(0, 0, which, part_i)
 
     def step(p, carry):
-        u, pair = pair_at(p)
+        u, pair = carry
         u_next, pair_next = pair_at(jnp.minimum(p + 1, STEPS - 1))
         h_next, c_next = u_next // 2, lax.rem(u_next, 2)
         pl.when((pair_next == 1) & (c_next == 0))(lambda: par_copy(h_next).wait_recv())
-        for at_step, h in ((6, 0), (16, 1), (23, 2)):
-            pl.when(p == at_step)(lambda h=h: serve(h))
+        for at_step, h in ((3, 0), (9, 1), (14, 2)):
+            pl.when((p == at_step) & inner)(lambda h=h: serve_z(h))
+        for at_step, h in ((5, 1), (11, 2)):
+            pl.when((p == at_step) & ~inner)(lambda h=h: start_rows(h))
+        for at_step, h in ((4, 0), (14, 1), (21, 2)):
+            pl.when(p == at_step)(lambda h=h: serve_rows(h))
 
         @pl.when((pair_next == 4) & (p < STEPS - 1) & (halo_at(c_next) > 0))
         def _():
             parcol_copy(h_next, c_next).wait_recv()
             pl.when(inner)(lambda: zcol_copy(h_next, c_next).wait_recv())
 
-        @pl.when(p == 17)
+        @pl.when(p == 15)
         def _():
             for zc in range(2):
                 for hop in (1, 3, 2):
                     w_copy(hop, zc).wait_recv()
                     w_forward(hop, zc).start()
 
-        for at_step, done in ((16, 0), (19, 1), (26, 2), (29, 3)):
+        for at_step, done in ((17, 0), (20, 1), (24, 2), (27, 3)):
             pl.when(p == at_step)(lambda done=done: forward(jnp.int32(done)))
+
+        @pl.when(p == STEPS - 2)
+        def _():
+            for zc in range(2):
+                w_own(zc).wait()
+                for hop in (1, 3, 2):
+                    w_forward(hop, zc).wait_recv()
+            project_first(0)
+
+        pl.when(p == STEPS - 1)(lambda: project_last(0, 0))
 
         pens = [pens_of(u, pair, which) for which in range(2)]
         c, h = lax.rem(u, 2), u // 2
@@ -367,26 +386,29 @@
                 )
                 score_step(u_next, pair_next, which, part_i)
 
-        @pl.when(pair == 4)
+        @pl.when((pair == 4) & (h < heads - 1))
         def _():
             ag[c, x, h] = (acc_ref[u] / l_ref[u]).T.astype(BF16)
             for way in range(2):
                 ag_copy(c, h, way).start()
 
-        return carry
-
-    lax.fori_loop(0, STEPS, step, 0)
-
-    for zc in range(2):
-        w_own(zc).wait()
-        for hop in (1, 3, 2):
-            w_forward(hop, zc).wait_recv()
-    project_first(0)
-    forward(jnp.int32(4))
+        @pl.when((pair == 4) & (h == heads - 1))
+        def _():
+            for b in range(parts):
+                at = slice(b * SUB, (b + 1) * SUB)
+                ag[c, x, heads - 1, at] = (acc_ref[u, :, at] / l_ref[u, :, at]).T.astype(BF16)
+                for hop in (1, 3, 2):
+                    end_copy(c, b, hop).start()
+
+        return u_next, pair_next
+
+    lax.fori_loop(0, STEPS, step, (jnp.int32(0), jnp.int32(0)))
+
+    project_last(0, 1)
     project_first(1)
-    forward(jnp.int32(5))
-    project_last(0)
-    project_last(1)
+    project_last(0, 2)
+    for b in range(parts):
+        project_last(1, b)
 
     for c in range(2):
         for b in range(tokens // SUB):
@@ -397,7 +419,9 @@
     for c in range(2):
         for b in range(tokens // SUB):
             sum_copy(c, b).wait_send()
-        for h in range(heads):
+            for hop in range(1, NX):
+                end_copy(c, b, hop).wait_send()
+        for h in range(heads - 1):
             ag_forward(c, h).wait_send()
             for way in range(2):
                 ag_copy(c, h, way).wait_send()
@@ -455,8 +479,9 @@
             dma((NX - 1, 2)), dma((NX - 1, 2)),
             dma((NX - 1, 2)), dma((NX - 1, 2)),
             dma((2,)),
-            dma((cols, heads, 2)), dma((cols, heads, 2)),
-            dma((cols, heads)), dma((cols, heads)),
+            dma((cols, heads - 1, 2)), dma((cols, heads - 1, 2)),
+            dma((cols, heads - 1)), dma((cols, heads - 1)),
+            dma((cols, blocks, NX - 1)), dma((cols, blocks, NX - 1)),
             dma((cols, blocks)), dma((cols, blocks)),
         ],
         compiler_params=pltpu.CompilerParams(

time: 111 us -> 103 us (0.928); the launches traced: 111 us -> 102 us
  Pallas kernels: 103 us -> 93.7 us
    pallas_call x1, Pallas kernels: 103 us -> 93.7 us  [layer(): pl.pallas_call(layer_kernel, in_specs=[pl.BlockSpec(memory_space=pltpu.SM...]
where the time goes in v4:
time: 103 us; the launch traced here: 102 us
  Pallas kernels  93.7 us (91%)
  local copies, waits for them, and re-layouts  6.5 us (6%)
  other arithmetic  1.63 us (2%)
    pallas_call x1, Pallas kernels, layer(): pl.pallas_call(layer_kernel, in_specs=[pl.BlockSpec(memory_space=pltpu.SM...  93.7 us
    reshape x3, local copies, waits for them, and re-layouts, tiled(): cut = block.reshape(frames, height, cols, TILE_W, heads, HEAD)  3.38 us
    transpose x1, local copies, waits for them, and re-layouts, untiled(): cut.transpose(1, 2, 0, 3, 4)  2.41 us

profile of v4, /device:TPU:17, one launch (start us, length us, event | category | flops | bytes accessed | tf_op | source)
XLA Modules:
  0.0 101.9 jit_solution(8187398940222269303)
XLA Ops:
  0.0 0.0 copy-start
  0.0 1.7 %copy.16 = bf16[12,8,2,8,3,128]{5,3,1,0,2,4:T(8,128)(2,1)S(1)} copy(bf16[12,8,2,8,3,128]{5,3,4,2,1,0:T(8,128)(2,1)} %bitcast.22) | data formatting | bytes 2359296 | tf_op jit(solution)/shard_map/reshape | solution.py:27
  1.7 0.0 copy-done
  1.7 0.3 copy.17
  2.1 0.0 copy-start.1
  2.1 1.6 %pad_maximum_fusion.kv_ref = bf16[3,2,2,768,128]{4,3,2,1,0:T(8,128)(2,1)} fusion(bf16[3,2,1,768,128]{4,3,2,1,0:T(8,128)(2,1)S(1)} %bitcast.21, bf16[3,2,1,768,128]{4,3,2,1,0:T(8,128)(2,1)S(1)} %bitcast.20), kind=kLoop, calls=%fused_computation | loop fusion | flops 1179648 | bytes 4718592 | tf_op jit(solution)/shard_map/stack | solution.py:500
  3.7 0.0 copy-done.1
  3.7 0.0 copy-start.2
  3.7 1.4 %copy.15 = bf16[12,8,2,8,3,128]{5,3,1,0,2,4:T(8,128)(2,1)} copy(bf16[12,8,2,8,3,128]{5,3,4,2,1,0:T(8,128)(2,1)S(1)} %bitcast.24) | data formatting | bytes 2359296 | tf_op jit(solution)/shard_map/reshape | solution.py:27
  5.1 0.0 copy-done.2
  5.1 0.1 copy.20
  5.2 0.6 reshape.24.radius
  5.8 93.7 %layer.1 = bf16[2,768,384]{2,1,0:T(8,128)(2,1)} custom-call(s32[6,2]{1,0:T(8,128)} %reshape.24.radius, bf16[3,2,768,128]{3,2,1,0:T(8,128)(2,1)} %bitcast.25, bf16[3,2,2,768,128]{4,3,2,1,0:T(8,128)(2,1)} %pad_maximum_fusion.kv_ref, bf16[256,384]{1,0:T(8,128)(2,1)} %tk_ref.1, bf16[256,384]{1,0:T(8,128)(2,1)} %tv_ref.1, bf16[384,3072]{1,0:T(8,128)(2,1)} %w_ref.1), custom_call_target="tpu_custom_call" | custom-call | flops 40000000000 | bytes 18000000 | tf_op jit(solution)/shard_map/layer/pallas_call | solution.py:450
  99.5 2.4 %copy.23 = bf16[12,8,2,8,384]{4,3,2,1,0:T(8,128)(2,1)} copy(bf16[12,8,2,8,384]{4,3,1,0,2:T(8,128)(2,1)} %bitcast.26) | data formatting | bytes 2359296 | tf_op jit(solution)/shard_map/transpose | solution.py:34
Async XLA Ops:
  0.0 1.7 %copy-start = (bf16[12,8,16,384]{3,2,1,0:T(8,128)(2,1)S(1)}, bf16[12,8,16,384]{3,2,1,0:T(8,128)(2,1)}, u32[]{:S(2)}) copy-start(bf16[12,8,16,384]{3,2,1,0:T(8,128)(2,1)} %param.9) | copy-start | bytes 3538948
  2.1 1.6 %copy-start.1 = (bf16[12,8,16,384]{3,2,1,0:T(8,128)(2,1)S(1)}, bf16[12,8,16,384]{3,2,1,0:T(8,128)(2,1)}, u32[]{:S(2)}) copy-start(bf16[12,8,16,384]{3,2,1,0:T(8,128)(2,1)} %param.7) | copy-start | bytes 3538948
  3.7 1.4 %copy-start.2 = (s32[3,2,1,2]{0,3,2,1:T(2,128)S(1)}, s32[3,2,1,2]{0,3,2,1:T(2,128)}, u32[]{:S(2)}) copy-start(s32[3,2,1,2]{0,3,2,1:T(2,128)} %param.12) | copy-start | bytes 148

commit v5 on v4

--- a/solution.py
+++ b/solution.py
@@ -67,20 +67,32 @@
 
 
 ORDER = (
-    (0, 0, 2), (1, 0, 2), (0, 2, 2), (1, 2, 2), (2, 0, 2), (0, 4, 1), (1, 4, 1), (2, 2, 1),
-    (3, 0, 2), (2, 3, 1), (3, 2, 2), (2, 4, 1), (3, 4, 1), (4, 0, 5), (5, 0, 5),
+    (0, 0, 2), (1, 0, 2), (2, 0, 2), (0, 2, 2), (1, 2, 2), (0, 4, 1), (1, 4, 1), (3, 0, 2),
+    (2, 2, 1), (4, 0, 2), (2, 3, 1), (3, 2, 2), (2, 4, 1), (3, 4, 1), (4, 2, 1), (5, 0, 2),
+    (4, 3, 1), (5, 2, 1), (4, 4, 1), (5, 3, 2),
 )
+STEP_LIST = [(unit, first + i) for unit, first, count in ORDER for i in range(count)]
 
 
 def pair_at(p):
-    unit, pair, start = jnp.int32(0), p, 0
-    for run_unit, first, count in ORDER:
+    code, start = p, 0
+    for unit, first, count in ORDER:
         if start > 0:
-            here = p >= start
-            unit = jnp.where(here, run_unit, unit)
-            pair = jnp.where(here, p + (first - start), pair)
+            code = jnp.where(p >= start, p + (8 * unit + first - start), code)
         start += count
-    return unit, pair
+    return code // 8, lax.rem(code, 8)
+
+
+def run_events(p, events, low, high):
+    if not any(low <= at < high for at in events):
+        return
+    if high - low == 1:
+        for act in events[low]:
+            act()
+        return
+    middle = (low + high) // 2
+    pl.when(p < middle)(lambda: run_events(p, events, low, middle))
+    pl.when(p >= middle)(lambda: run_events(p, events, middle, high))
 
 
 STEPS = 30
@@ -204,12 +216,6 @@
     for step in range(1, NX):
         greet({"hd": x_at(step)})
     greet({"hd": lax.rem(hd + NX, 2 * NX)})
-    pl.semaphore_wait(
-        barrier,
-        2 + NX - 1
-        + has_left.astype(jnp.int32) + has_right.astype(jnp.int32) + inner.astype(jnp.int32),
-    )
-
     def when_side(side, act):
         pl.when(has_right if side == 0 else has_left)(act)
 
@@ -220,14 +226,6 @@
         for side in range(2):
             when_side(side, lambda side=side: row_copy(h, side).start())
 
-    start_rows(0)
-    for h in range(heads):
-        pl.when(inner)(lambda h=h: z_copy(h).start())
-        par_copy(h).start()
-    for zc in range(2):
-        w_own(zc).start()
-        for step in (1, 3, 2):
-            w_copy(step, zc).start()
     for h in range(heads):
         kvh[h, 5:7] = kv_ref[h]
         lanes = slice(h * HEAD, (h + 1) * HEAD)
@@ -244,6 +242,21 @@
     l_ref[...] = jnp.zeros_like(l_ref)
     acc_ref[...] = jnp.zeros_like(acc_ref)
 
+    pl.semaphore_wait(
+        barrier,
+        2 + NX - 1
+        + has_left.astype(jnp.int32) + has_right.astype(jnp.int32) + inner.astype(jnp.int32),
+    )
+
+    start_rows(0)
+    for h in range(heads):
+        pl.when(inner)(lambda h=h: z_copy(h).start())
+        par_copy(h).start()
+    for zc in range(2):
+        w_own(zc).start()
+        for step in (1, 3, 2):
+            w_copy(step, zc).start()
+
     def serve_z(h):
         z_copy(h).wait_recv()
         for side in range(2):
@@ -293,16 +306,16 @@
             for qt in range(2):
                 ok = (
                     there
-                    & (away <= radius[2 + qt, c])
-                    & (gap <= radius[4 + qt, c])
-                    & (abs(qt - kt) <= radius[qt, c])
+                    & (away <= radius[1, qt, 0, c])
+                    & (gap <= radius[2, qt, 0, c])
+                    & (abs(qt - kt) <= radius[0, qt, 0, c])
                 )
                 pen.append(jnp.where(chunk == 0, LOG3, jnp.where(ok, 0.0, FAR)))
             pens.append(jnp.where(late, pen[1], pen[0]))
         return pens
 
     def forward(u):
-        h, c = u // 2, lax.rem(u, 2)
+        h, c = u // 2, u % 2
         ag_copy(c, h, c).wait_recv()
         ag_forward(c, h).start()
 
@@ -338,42 +351,45 @@
         for part_i in range(parts):
             score_step(0, 0, which, part_i)
 
+    events = {}
+
+    def plan(at_step, act, *given):
+        events.setdefault(at_step, []).append(lambda: act(*given))
+
+    def await_pair(unit, pair):
+        h, c = unit // 2, unit % 2
+        if pair == 1 and c == 0:
+            par_copy(h).wait_recv()
+        if pair == 4:
+
+            @pl.when(has_left if c == 0 else has_right)
+            def _():
+                parcol_copy(h, c).wait_recv()
+                pl.when(inner)(lambda: zcol_copy(h, c).wait_recv())
+
+    def pass_weights():
+        for zc in range(2):
+            for hop in (1, 3, 2):
+                w_copy(hop, zc).wait_recv()
+                w_forward(hop, zc).start()
+
+    for at_step, h in ((5, 0), (12, 1), (18, 2)):
+        plan(at_step, lambda h: pl.when(inner)(lambda: serve_z(h)), h)
+    for at_step, h in ((8, 1), (17, 2)):
+        plan(at_step, lambda h: pl.when(~inner)(lambda: start_rows(h)), h)
+    for at_step, h in ((6, 0), (16, 1), (24, 2)):
+        plan(at_step, serve_rows, h)
+    plan(13, pass_weights)
+    for at_step, done in ((18, 0), (23, 1), (28, 2)):
+        plan(at_step, forward, done)
+    for at_step, ahead in enumerate(STEP_LIST[1:]):
+        if ahead[1] == 4 or (ahead[1] == 1 and ahead[0] % 2 == 0):
+            plan(at_step, await_pair, *ahead)
+
     def step(p, carry):
         u, pair = carry
         u_next, pair_next = pair_at(jnp.minimum(p + 1, STEPS - 1))
-        h_next, c_next = u_next // 2, lax.rem(u_next, 2)
-        pl.when((pair_next == 1) & (c_next == 0))(lambda: par_copy(h_next).wait_recv())
-        for at_step, h in ((3, 0), (9, 1), (14, 2)):
-            pl.when((p == at_step) & inner)(lambda h=h: serve_z(h))
-        for at_step, h in ((5, 1), (11, 2)):
-            pl.when((p == at_step) & ~inner)(lambda h=h: start_rows(h))
-        for at_step, h in ((4, 0), (14, 1), (21, 2)):
-            pl.when(p == at_step)(lambda h=h: serve_rows(h))
-
-        @pl.when((pair_next == 4) & (p < STEPS - 1) & (halo_at(c_next) > 0))
-        def _():
-            parcol_copy(h_next, c_next).wait_recv()
-            pl.when(inner)(lambda: zcol_copy(h_next, c_next).wait_recv())
-
-        @pl.when(p == 15)
-        def _():
-            for zc in range(2):
-                for hop in (1, 3, 2):
-                    w_copy(hop, zc).wait_recv()
-                    w_forward(hop, zc).start()
-
-        for at_step, done in ((17, 0), (20, 1), (24, 2), (27, 3)):
-            pl.when(p == at_step)(lambda done=done: forward(jnp.int32(done)))
-
-        @pl.when(p == STEPS - 2)
-        def _():
-            for zc in range(2):
-                w_own(zc).wait()
-                for hop in (1, 3, 2):
-                    w_forward(hop, zc).wait_recv()
-            project_first(0)
-
-        pl.when(p == STEPS - 1)(lambda: project_last(0, 0))
+        run_events(p, events, 0, STEPS)
 
         pens = [pens_of(u, pair, which) for which in range(2)]
         c, h = lax.rem(u, 2), u // 2
@@ -404,9 +420,16 @@
 
     lax.fori_loop(0, STEPS, step, (jnp.int32(0), jnp.int32(0)))
 
-    project_last(0, 1)
+    for zc in range(2):
+        w_own(zc).wait()
+        for hop in (1, 3, 2):
+            w_forward(hop, zc).wait_recv()
+    forward(3)
+    project_first(0)
+    project_last(0, 0)
     project_first(1)
-    project_last(0, 2)
+    for b in range(1, parts):
+        project_last(0, b)
     for b in range(parts):
         project_last(1, b)
 
@@ -498,8 +521,7 @@
     n_frames, height, _, _ = queries.shape
     q = tiled(queries)
     kv = jnp.stack([tiled(video_keys), tiled(video_values)], axis=2)
-    radius = tile_radius[:, :, 0, :].reshape(6, -1)
-    return untiled(layer(radius, q, kv, text_keys, text_values, out_weight), n_frames, height)
+    return untiled(layer(tile_radius, q, kv, text_keys, text_values, out_weight), n_frames, height)
 
 
 def solution(mesh):

time: 103 us -> 114 us (1.11)
  Pallas kernels: 93.7 us -> 105 us
    pallas_call x1, Pallas kernels: 93.7 us -> 105 us  [layer(): pl.pallas_call(layer_kernel, in_specs=[pl.BlockSpec(memory_space=pltpu.SM...]
where the time goes in v5:
time: 114 us
  Pallas kernels  105 us (92%)
  local copies, waits for them, and re-layouts  6.49 us (6%)
  other arithmetic  1.63 us (1%)
    pallas_call x1, Pallas kernels, layer(): pl.pallas_call(layer_kernel, in_specs=[pl.BlockSpec(memory_space=pltpu.SM...  105 us
    reshape x3, local copies, waits for them, and re-layouts, tiled(): cut = block.reshape(frames, height, cols, TILE_W, heads, HEAD)  3.38 us
    transpose x1, local copies, waits for them, and re-layouts, untiled(): cut.transpose(1, 2, 0, 3, 4)  2.41 us

profile of v5, /device:TPU:17, one launch (start us, length us, event | category | flops | bytes accessed | tf_op | source)
XLA Modules:
  0.0 113.6 jit_solution(10101297004613526108)
XLA Ops:
  0.0 0.0 copy-start
  0.0 1.7 %copy.9 = bf16[12,8,2,8,3,128]{5,3,1,0,2,4:T(8,128)(2,1)S(1)} copy(bf16[12,8,2,8,3,128]{5,3,4,2,1,0:T(8,128)(2,1)} %bitcast.20) | data formatting | bytes 2359296 | tf_op jit(solution)/shard_map/reshape | solution.py:27
  1.7 0.0 copy-done
  1.7 0.3 copy.10
  2.1 0.0 copy-start.1
  2.1 1.6 %pad_maximum_fusion.kv_ref = bf16[3,2,2,768,128]{4,3,2,1,0:T(8,128)(2,1)} fusion(bf16[3,2,1,768,128]{4,3,2,1,0:T(8,128)(2,1)S(1)} %bitcast.19, bf16[3,2,1,768,128]{4,3,2,1,0:T(8,128)(2,1)S(1)} %bitcast.18), kind=kLoop, calls=%fused_computation | loop fusion | flops 1179648 | bytes 4718592 | tf_op jit(solution)/shard_map/stack | solution.py:523
  3.7 0.0 copy-done.1
  3.7 0.0 copy-start.2
  3.7 1.4 %copy.8 = bf16[12,8,2,8,3,128]{5,3,1,0,2,4:T(8,128)(2,1)} copy(bf16[12,8,2,8,3,128]{5,3,4,2,1,0:T(8,128)(2,1)S(1)} %bitcast.22) | data formatting | bytes 2359296 | tf_op jit(solution)/shard_map/reshape | solution.py:27
  5.1 0.0 copy-done.2
  5.1 0.7 copy.11.radius
  5.7 105.5 %layer.1 = bf16[2,768,384]{2,1,0:T(8,128)(2,1)} custom-call(s32[3,2,1,2]{3,2,1,0:T(1,128)} %copy.11.radius, bf16[3,2,768,128]{3,2,1,0:T(8,128)(2,1)} %bitcast.24, bf16[3,2,2,768,128]{4,3,2,1,0:T(8,128)(2,1)} %pad_maximum_fusion.kv_ref, bf16[256,384]{1,0:T(8,128)(2,1)} %tk_ref.1, bf16[256,384]{1,0:T(8,128)(2,1)} %tv_ref.1, bf16[384,3072]{1,0:T(8,128)(2,1)} %w_ref.1), custom_call_target="tpu_custom_call" | custom-call | flops 40000000000 | bytes 18000000 | tf_op jit(solution)/shard_map/layer/pallas_call | solution.py:473
  111.2 2.4 %copy.14 = bf16[12,8,2,8,384]{4,3,2,1,0:T(8,128)(2,1)} copy(bf16[12,8,2,8,384]{4,3,1,0,2:T(8,128)(2,1)} %bitcast.23) | data formatting | bytes 2359296 | tf_op jit(solution)/shard_map/transpose | solution.py:34
Async XLA Ops:
  0.0 1.7 %copy-start = (bf16[12,8,16,384]{3,2,1,0:T(8,128)(2,1)S(1)}, bf16[12,8,16,384]{3,2,1,0:T(8,128)(2,1)}, u32[]{:S(2)}) copy-start(bf16[12,8,16,384]{3,2,1,0:T(8,128)(2,1)} %param.9) | copy-start | bytes 3538948
  2.1 1.6 %copy-start.1 = (bf16[12,8,16,384]{3,2,1,0:T(8,128)(2,1)S(1)}, bf16[12,8,16,384]{3,2,1,0:T(8,128)(2,1)}, u32[]{:S(2)}) copy-start(bf16[12,8,16,384]{3,2,1,0:T(8,128)(2,1)} %param.7) | copy-start | bytes 3538948
  3.7 1.4 %copy-start.2 = (s32[3,2,1,2]{0,3,2,1:T(2,128)S(1)}, s32[3,2,1,2]{0,3,2,1:T(2,128)}, u32[]{:S(2)}) copy-start(s32[3,2,1,2]{0,3,2,1:T(2,128)} %param.12) | copy-start | bytes 148

commit v6 on v5

--- a/solution.py
+++ b/solution.py
@@ -66,11 +66,7 @@
     m_ref[:, at] = m_new
 
 
-ORDER = (
-    (0, 0, 2), (1, 0, 2), (2, 0, 2), (0, 2, 2), (1, 2, 2), (0, 4, 1), (1, 4, 1), (3, 0, 2),
-    (2, 2, 1), (4, 0, 2), (2, 3, 1), (3, 2, 2), (2, 4, 1), (3, 4, 1), (4, 2, 1), (5, 0, 2),
-    (4, 3, 1), (5, 2, 1), (4, 4, 1), (5, 3, 2),
-)
+ORDER = ((0, 0, 2), (1, 0, 2), (2, 0, 2), (0, 2, 2), (1, 2, 2), (0, 4, 1), (1, 4, 1), (3, 0, 2), (2, 2, 2), (3, 2, 2), (2, 4, 1), (3, 4, 1), (4, 0, 5), (5, 0, 5))
 STEP_LIST = [(unit, first + i) for unit, first, count in ORDER for i in range(count)]
 
 
@@ -373,18 +369,29 @@
                 w_copy(hop, zc).wait_recv()
                 w_forward(hop, zc).start()
 
-    for at_step, h in ((5, 0), (12, 1), (18, 2)):
+    for at_step, h in ((4, 0), (10, 1), (15, 2)):
         plan(at_step, lambda h: pl.when(inner)(lambda: serve_z(h)), h)
-    for at_step, h in ((8, 1), (17, 2)):
+    for at_step, h in ((7, 1), (14, 2)):
         plan(at_step, lambda h: pl.when(~inner)(lambda: start_rows(h)), h)
-    for at_step, h in ((6, 0), (16, 1), (24, 2)):
+    for at_step, h in ((5, 0), (14, 1), (21, 2)):
         plan(at_step, serve_rows, h)
-    plan(13, pass_weights)
-    for at_step, done in ((18, 0), (23, 1), (28, 2)):
+    plan(12, pass_weights)
+    for at_step, done in ((15, 0), (18, 1), (23, 2), (26, 3)):
         plan(at_step, forward, done)
     for at_step, ahead in enumerate(STEP_LIST[1:]):
         if ahead[1] == 4 or (ahead[1] == 1 and ahead[0] % 2 == 0):
             plan(at_step, await_pair, *ahead)
+
+    def weights_here():
+        for zc in range(2):
+            w_own(zc).wait()
+            for hop in (1, 3, 2):
+                w_forward(hop, zc).wait_recv()
+        project_first(0)
+
+    plan(27, weights_here)
+    plan(28, project_last, 0, 0)
+    plan(29, project_last, 0, 1)
 
     def step(p, carry):
         u, pair = carry
@@ -420,16 +427,8 @@
 
     lax.fori_loop(0, STEPS, step, (jnp.int32(0), jnp.int32(0)))
 
-    for zc in range(2):
-        w_own(zc).wait()
-        for hop in (1, 3, 2):
-            w_forward(hop, zc).wait_recv()
-    forward(3)
-    project_first(0)
-    project_last(0, 0)
+    project_last(0, 2)
     project_first(1)
-    for b in range(1, parts):
-        project_last(0, b)
     for b in range(parts):
         project_last(1, b)
 

time: 114 us -> 98 us (0.86)
  Pallas kernels: 105 us -> 89.3 us
    pallas_call x1, Pallas kernels: 105 us -> 89.3 us  [layer(): pl.pallas_call(layer_kernel, in_specs=[pl.BlockSpec(memory_space=pltpu.SM...]
where the time goes in v6:
time: 98 us; the launch traced here: 97.4 us
  Pallas kernels  89.3 us (91%)
  local copies, waits for them, and re-layouts  6.49 us (7%)
  other arithmetic  1.63 us (2%)
    pallas_call x1, Pallas kernels, layer(): pl.pallas_call(layer_kernel, in_specs=[pl.BlockSpec(memory_space=pltpu.SM...  89.3 us
    reshape x3, local copies, waits for them, and re-layouts, tiled(): cut = block.reshape(frames, height, cols, TILE_W, heads, HEAD)  3.38 us
    transpose x1, local copies, waits for them, and re-layouts, untiled(): cut.transpose(1, 2, 0, 3, 4)  2.41 us

profile of v6, /device:TPU:17, one launch (start us, length us, event | category | flops | bytes accessed | tf_op | source)
XLA Modules:
  0.0 97.4 jit_solution(14156361296365624313)
XLA Ops:
  0.0 0.0 copy-start
  0.0 1.7 %copy.9 = bf16[12,8,2,8,3,128]{5,3,1,0,2,4:T(8,128)(2,1)S(1)} copy(bf16[12,8,2,8,3,128]{5,3,4,2,1,0:T(8,128)(2,1)} %bitcast.20) | data formatting | bytes 2359296 | tf_op jit(solution)/shard_map/reshape | solution.py:27
  1.7 0.0 copy-done
  1.7 0.3 copy.10
  2.1 0.0 copy-start.1
  2.1 1.6 %pad_maximum_fusion.kv_ref = bf16[3,2,2,768,128]{4,3,2,1,0:T(8,128)(2,1)} fusion(bf16[3,2,1,768,128]{4,3,2,1,0:T(8,128)(2,1)S(1)} %bitcast.19, bf16[3,2,1,768,128]{4,3,2,1,0:T(8,128)(2,1)S(1)} %bitcast.18), kind=kLoop, calls=%fused_computation | loop fusion | flops 1179648 | bytes 4718592 | tf_op jit(solution)/shard_map/stack | solution.py:522
  3.7 0.0 copy-done.1
  3.7 0.0 copy-start.2
  3.7 1.4 %copy.8 = bf16[12,8,2,8,3,128]{5,3,1,0,2,4:T(8,128)(2,1)} copy(bf16[12,8,2,8,3,128]{5,3,4,2,1,0:T(8,128)(2,1)S(1)} %bitcast.22) | data formatting | bytes 2359296 | tf_op jit(solution)/shard_map/reshape | solution.py:27
  5.1 0.0 copy-done.2
  5.1 0.7 copy.11.radius
  5.7 89.3 %layer.1 = bf16[2,768,384]{2,1,0:T(8,128)(2,1)} custom-call(s32[3,2,1,2]{3,2,1,0:T(1,128)} %copy.11.radius, bf16[3,2,768,128]{3,2,1,0:T(8,128)(2,1)} %bitcast.24, bf16[3,2,2,768,128]{4,3,2,1,0:T(8,128)(2,1)} %pad_maximum_fusion.kv_ref, bf16[256,384]{1,0:T(8,128)(2,1)} %tk_ref.1, bf16[256,384]{1,0:T(8,128)(2,1)} %tv_ref.1, bf16[384,3072]{1,0:T(8,128)(2,1)} %w_ref.1), custom_call_target="tpu_custom_call" | custom-call | flops 40000000000 | bytes 18000000 | tf_op jit(solution)/shard_map/layer/pallas_call | solution.py:472
  95.0 2.4 %copy.14 = bf16[12,8,2,8,384]{4,3,2,1,0:T(8,128)(2,1)} copy(bf16[12,8,2,8,384]{4,3,1,0,2:T(8,128)(2,1)} %bitcast.23) | data formatting | bytes 2359296 | tf_op jit(solution)/shard_map/transpose | solution.py:34
Async XLA Ops:
  0.0 1.7 %copy-start = (bf16[12,8,16,384]{3,2,1,0:T(8,128)(2,1)S(1)}, bf16[12,8,16,384]{3,2,1,0:T(8,128)(2,1)}, u32[]{:S(2)}) copy-start(bf16[12,8,16,384]{3,2,1,0:T(8,128)(2,1)} %param.9) | copy-start | bytes 3538948
  2.1 1.6 %copy-start.1 = (bf16[12,8,16,384]{3,2,1,0:T(8,128)(2,1)S(1)}, bf16[12,8,16,384]{3,2,1,0:T(8,128)(2,1)}, u32[]{:S(2)}) copy-start(bf16[12,8,16,384]{3,2,1,0:T(8,128)(2,1)} %param.7) | copy-start | bytes 3538948
  3.7 1.4 %copy-start.2 = (s32[3,2,1,2]{0,3,2,1:T(2,128)S(1)}, s32[3,2,1,2]{0,3,2,1:T(2,128)}, u32[]{:S(2)}) copy-start(s32[3,2,1,2]{0,3,2,1:T(2,128)} %param.12) | copy-start | bytes 148
